TPU v7x, 256 devices: a whole 4x4x8 slice. The times are simulated.
256 devices in a mesh: dp: 16 (over z, core), row: 8 (over x_lo, y), col: 2 (over x_hi).
Axes of the slice: x: 4 (x_hi: 2, x_lo: 2; x = x_hi * 2 + x_lo), y: 4, z: 8, core: 2. Of those that a mesh axis runs over, the one named last changes fastest.
Arguments:
- patches: bfloat16 [32768, 1408], P(('dp', 'row', 'col')), may hold values from -6 to 6
- norm_gain: float32 [1408], replicated, may hold values from 0.5 to 1.5
- norm_bias: float32 [1408], replicated, may hold values from -3 to 3
- up_weight: bfloat16 [1408, 6144], P('col', 'row'), may hold values from -0.15625 to 0.15625
- up_bias: float32 [6144], P('row'), may hold values from -3 to 3
- down_weight: bfloat16 [6144, 1408], P('row', 'col'), may hold values from -0.078125 to 0.078125
- down_bias: float32 [1408], replicated, may hold values from -3 to 3
- cotangent: bfloat16 [32768, 1408], P(('dp', 'row', 'col')), may hold values from -24 to 24
Outputs:
- output: float32 [32768, 1408], P(('dp', 'row', 'col'))
- patch_grad: float32 [32768, 1408], P(('dp', 'row', 'col'))
- up_grad: float32 [1408, 6144], P('col', 'row')
- down_grad: float32 [6144, 1408], P('row', 'col')
- bias_grad: float32 [6144], P('row')
- norm_grad: float32 [2, 1408], replicated
All inputs are finite; a program needn't handle non-finite values.
Results may differ from a plain program's by a relative error of at most 0.0055.
Values may be sent and summed in bfloat16 or wider, within the bound.
A program may use at most 128 MiB of HBM per device.

v0:
```python
import functools
import math

import jax
import jax.numpy as jnp
from jax import lax
from jax.sharding import Mesh
from jax.sharding import PartitionSpec as P

ROW = ("row_0", "row_1")
DP = ("dp_0", "dp_1")
DP_COL = ("dp_0", "dp_1", "col")
DP_ROW_COL = ("dp_0", "dp_1", "row_0", "row_1", "col")


EPSILON = 1e-06
GELU_ROOT = 0.7978845608028654
GELU_CUBIC = 0.044715


def in_order(tiles, dim):
    tiles = jnp.moveaxis(tiles, 0, dim)
    shape = tiles.shape
    return tiles.reshape(*shape[:dim], shape[dim] * shape[dim + 1], *shape[dim + 2 :])


def from_everyone(array, axis):
    copies = jnp.broadcast_to(array, (lax.axis_size(axis), *array.shape))
    return lax.all_to_all(copies, axis, split_axis=0, concat_axis=0, tiled=True)


def collect(array, axis, dim):
    return in_order(from_everyone(array, axis), dim)


def cut_along(array, dim, peers):
    shape = array.shape
    tiles = array.reshape(*shape[:dim], peers, shape[dim] // peers, *shape[dim + 1 :])
    return jnp.moveaxis(tiles, dim, 0)


def sum_at_owner(array, axis, dim):
    peers = lax.axis_size(axis)
    tiles = lax.all_to_all(cut_along(array, dim, peers), axis, 0, 0, tiled=True)
    return jnp.sum(tiles, axis=0)


def packed_total(arrays, axis):
    ends = [0]
    for a in arrays:
        ends.append(ends[-1] + a.size)
    total = lax.psum(jnp.concatenate([a.ravel() for a in arrays]), axis)
    return tuple((total[b:e].reshape(a.shape) for a, b, e in zip(arrays, ends, ends[1:])))


def over_copies(array, axis):
    return from_everyone(array, axis).sum(axis=0)


def own_block(tiles, axes, turns):
    shape = [lax.axis_size(a) for a in axes]
    tiles = tiles.reshape(*shape, *tiles.shape[1:])
    tiles = tiles.transpose(*turns, *range(len(axes), tiles.ndim))
    tiles = tiles.reshape(-1, *tiles.shape[len(axes) :])
    for k in turns:
        tiles = lax.psum_scatter(tiles, axes[k], scatter_dimension=0, tiled=True)
    return tiles[0]


def scatter_axes(array, axes, turns, dim):
    peers = lax.axis_size(axes)
    return own_block(cut_along(array, dim, peers), axes, turns)


def over_axes(array, axes):
    return functools.reduce(lax.psum, axes, array)


def gelu_value(value):
    inner = jnp.tanh(GELU_ROOT * (value + GELU_CUBIC * value * value * value))
    return 0.5 * value * (1.0 + inner)


def gelu_slope(value):
    inner = jnp.tanh(GELU_ROOT * (value + GELU_CUBIC * value * value * value))
    return 0.5 * (1.0 + inner) + 0.5 * value * (1.0 - inner * inner) * GELU_ROOT * (
        1.0 + 3.0 * GELU_CUBIC * value * value
    )


def contract_rows(left, right):
    return lax.dot_general(
        left, right, (((0,), (0,)), ((), ())), preferred_element_type=jnp.float32
    )


def contract_cols(left, right):
    return lax.dot_general(
        left, right, (((1,), (1,)), ((), ())), preferred_element_type=jnp.float32
    )


def on_device(patches, norm_gain, norm_bias, up_weight, up_bias, down_weight, down_bias, cotangent):
    n_row = lax.axis_size(ROW)
    n_col = lax.axis_size("col")
    n_replica = lax.axis_size(DP)
    local_rows = patches.shape[0]
    scaling = 1.0 / math.sqrt(local_rows * n_row * n_col * n_replica)
    wide_patches = patches.astype(jnp.float32)
    centred = wide_patches - jnp.mean(wide_patches, axis=1, keepdims=True)
    inverse_spread = lax.rsqrt(jnp.mean(centred * centred, axis=1, keepdims=True) + EPSILON)
    standard = centred * inverse_spread
    normed = (standard * norm_gain + norm_bias).astype(jnp.bfloat16)
    up_full = collect(up_weight, "col", 0)
    normed_rows = lax.all_gather(normed, ROW, axis=0, tiled=True)
    preact = jnp.dot(normed_rows, up_full, preferred_element_type=jnp.float32) + up_bias
    activated = gelu_value(preact).astype(jnp.bfloat16)
    down_full = collect(down_weight, "col", 1)
    projected = lax.psum_scatter(
        jnp.dot(activated, down_full, preferred_element_type=jnp.float32),
        ROW,
        scatter_dimension=0,
        tiled=True,
    )
    output = projected + down_bias + wide_patches
    upstream = lax.all_gather(cotangent, ROW, axis=0, tiled=True)
    down_partial = contract_rows(activated, upstream)
    down_grad = sum_at_owner(down_partial, "col", 1)
    slope = (contract_cols(upstream, down_full) * gelu_slope(preact)).astype(jnp.bfloat16)
    full_grad = contract_rows(normed_rows, slope)
    up_grad = sum_at_owner(full_grad, "col", 0)
    up_grad, down_grad = packed_total((up_grad, down_grad), DP)
    bias_grad = over_copies(jnp.sum(slope.astype(jnp.float32), axis=0), DP_COL)
    normed_back = scatter_axes(contract_cols(slope, up_full), ROW, (1, 0), 0)
    norm_terms = jnp.stack([jnp.sum(normed_back * standard, axis=0), jnp.sum(normed_back, axis=0)])
    norm_grad = over_axes(norm_terms, DP_ROW_COL)
    scaled = normed_back * norm_gain
    back = inverse_spread * (
        scaled
        - jnp.mean(scaled, axis=1, keepdims=True)
        - standard * jnp.mean(scaled * standard, axis=1, keepdims=True)
    )
    patch_grad = back + cotangent.astype(jnp.float32)
    return (
        output,
        patch_grad,
        up_grad * scaling,
        down_grad * scaling,
        bias_grad * scaling,
        norm_grad * scaling,
    )


def solution(mesh):
    split = Mesh(
        mesh.devices.reshape(8, 2, 2, 4, mesh.shape["col"]),
        ("dp_0", "dp_1", "row_0", "row_1", "col"),
    )
    placed = (
        P(DP_ROW_COL, None),
        P(),
        P(),
        P("col", ROW),
        P(ROW),
        P(ROW, "col"),
        P(),
        P(DP_ROW_COL, None),
    )
    return jax.shard_map(
        on_device,
        mesh=split,
        in_specs=placed,
        out_specs=(
            P(DP_ROW_COL, None),
            P(DP_ROW_COL, None),
            P("col", ROW),
            P(ROW, "col"),
            P(ROW),
            P(),
        ),
        check_vma=False,
    )
```

profile of v0, /device:TPU:7, one launch (start us, length us, event | category | flops | bytes accessed | tf_op | source)
XLA Modules:
  0.0 518.8 jit_solution(7841110046638156075)
XLA Ops:
  7.2 1.1 convert_reduce_fusion.1
  8.3 1.2 fusion.20
  9.6 2.0 fusion.14
  11.7 0.7 all-gather.5.cloned.1.call-update
  12.4 1.5 broadcast_in_dim.6
  13.9 42.4 %all_to_all.26 = bf16[2,704,768]{2,1,0:T(8,128)(2,1)} all-to-all(bf16[2,704,768]{2,1,0:T(8,128)(2,1)S(1)} %broadcast_in_dim.6), channel_id=1, replica_groups=mesh['dp_0'=8,'dp_1'=2,'row_0'=2,'row_1'=4,'col'=2] {'col'}, dimensions={0} | all-to-all | bytes 4325376 | tf_op jit(solution)/shard_map/all_to_all | solution.py:29
  56.3 1.5 broadcast_in_dim.7
  57.8 7.3 %all-to-all-start.1 = ((bf16[2,768,704]{1,2,0:T(8,128)(2,1)}), bf16[2,768,704]{1,2,0:T(8,128)(2,1)S(1)}, u32[]{:S(2)}, u32[]{:S(2)}) async-start(bf16[2,768,704]{1,2,0:T(8,128)(2,1)} %broadcast_in_dim.7), calls=%async_computation.1 | async-start | bytes 4325376 | tf_op jit(solution)/shard_map/all_to_all | solution.py:29
  65.1 10.2 %all-gather.3.cloned.1.call-done = bf16[1024,1408]{1,0:T(8,128)(2,1)} async-done(((bf16[128,1408]{1,0:T(8,128)(2,1)}), bf16[1024,1408]{1,0:T(8,128)(2,1)}) %all-gather.3.cloned.1.call-update) | async-done | bytes 2883600 | tf_op jit(solution)/shard_map/all_gather | solution.py:115
  75.3 6.8 %fusion.24 = f32[1024,768]{1,0:T(8,128)} fusion(bf16[1024,1408]{1,0:T(8,128)(2,1)} %all-gather.3.cloned.1.call-done, bf16[1408,768]{1,0:T(8,128)(2,1)} %bitcast.40), kind=kOutput, calls=%fused_computation.43 | convolution fusion | flops 2214592512 | bytes 8192000 | tf_op jit(solution)/shard_map/dot_general | solution.py:116
  82.0 11.8 %all-to-all-done.1 = bf16[2,768,704]{1,2,0:T(8,128)(2,1)S(1)} async-done(((bf16[2,768,704]{1,2,0:T(8,128)(2,1)}), bf16[2,768,704]{1,2,0:T(8,128)(2,1)S(1)}, u32[]{:S(2)}, u32[]{:S(2)}) %all-to-all-start.1) | async-done | bytes 2162720 | tf_op jit(solution)/shard_map/all_to_all | solution.py:29
  93.8 28.3 %all-gather.5.cloned.1.call-done = bf16[1024,1408]{1,0:T(8,128)(2,1)} async-done(((bf16[128,1408]{1,0:T(8,128)(2,1)}), bf16[1024,1408]{1,0:T(8,128)(2,1)}) %all-gather.5.cloned.1.call-update) | async-done | bytes 2883600 | tf_op jit(solution)/shard_map/all_gather | solution.py:126
  122.1 6.9 %convert_reduce_fusion = (f32[768]{0:T(1024)S(1)}, bf16[1024,768]{1,0:T(8,128)(2,1)S(1)}) fusion(f32[1024,768]{1,0:T(8,128)} %fusion.24, f32[768]{0:T(1024)S(1)} %copy-done.9, bf16[1024,1408]{1,0:T(8,128)(2,1)} %all-gather.5.cloned.1.call-done, bf16[768,1408]{0,1:T(8,128)(2,1)S(1)} %bitcast.38), kind=kOutput, calls=%fused_computation.11 | convolution fusion | flops 2231893248 | bytes 9771008 | tf_op jit(solution)/shard_map/dot_general | solution.py:98
  129.1 4.5 fusion.25
  133.6 5.8 %all-to-all-start.2 = ((f32[2,704,768]{2,1,0:T(8,128)}), f32[2,704,768]{2,1,0:T(8,128)}, u32[]{:S(2)}, u32[]{:S(2)}) async-start(f32[2,704,768]{2,1,0:T(8,128)} %bitcast.37), calls=%async_computation.5 | async-start | bytes 8650752 | tf_op jit(solution)/shard_map/all_to_all | solution.py:44
  139.5 7.5 %fusion.22 = f32[768,1408]{0,1:T(8,128)} fusion(bf16[1024,1408]{1,0:T(8,128)(2,1)} %all-gather.5.cloned.1.call-done, f32[1024,768]{1,0:T(8,128)} %fusion.24, f32[768]{0:T(1024)S(1)} %copy-done.9), kind=kOutput, calls=%fused_computation.41 | convolution fusion | flops 2222456832 | bytes 10357760 | tf_op jit(solution)/shard_map/dot_general | solution.py:92
  147.0 36.1 %all-to-all-done.2 = f32[2,704,768]{2,1,0:T(8,128)} async-done(((f32[2,704,768]{2,1,0:T(8,128)}), f32[2,704,768]{2,1,0:T(8,128)}, u32[]{:S(2)}, u32[]{:S(2)}) %all-to-all-start.2) | async-done | bytes 4325408 | tf_op jit(solution)/shard_map/all_to_all | solution.py:44
  183.2 8.6 %all-to-all-start.3 = ((f32[2,768,704]{1,2,0:T(8,128)}), f32[2,768,704]{1,2,0:T(8,128)}, u32[]{:S(2)}, u32[]{:S(2)}) async-start(f32[2,768,704]{1,2,0:T(8,128)} %bitcast.36), calls=%async_computation.6 | async-start | bytes 8650752 | tf_op jit(solution)/shard_map/all_to_all | solution.py:44
  191.8 4.0 convolution_bitcast_fusion
  195.8 2.9 copy.27
  198.8 2.7 reduce_sum.94
  201.5 1.5 reshape.88
  203.0 31.6 %all-to-all-done.3 = f32[2,768,704]{1,2,0:T(8,128)} async-done(((f32[2,768,704]{1,2,0:T(8,128)}), f32[2,768,704]{1,2,0:T(8,128)}, u32[]{:S(2)}, u32[]{:S(2)}) %all-to-all-start.3) | async-done | bytes 4325408 | tf_op jit(solution)/shard_map/all_to_all | solution.py:44
  234.6 4.1 reduce_sum.95
  238.7 2.0 copy.29
  240.7 2.5 reshape.90
  243.2 4.3 pad_maximum_fusion
  247.6 19.9 %reduce-scatter.6.cloned.1.call-done = f32[2,128,1408]{2,1,0:T(8,128)} async-done(((f32[8,128,1408]{2,1,0:T(8,128)}), f32[2,128,1408]{2,1,0:T(8,128)}) %reduce-scatter.6.cloned.1.call-update) | async-done | bytes 1441808 | tf_op jit(solution)/shard_map/reduce_scatter | solution.py:66
  267.5 0.7 broadcast_in_dim.8
  268.2 10.5 %all-to-all-start.4 = ((f32[32,1,768]{2,1,0:T(1,128)}), f32[32,1,768]{2,1,0:T(1,128)S(1)}, u32[]{:S(2)}, u32[]{:S(2)}) async-start(f32[32,1,768]{2,1,0:T(1,128)} %broadcast_in_dim.8), calls=%async_computation.7 | async-start | bytes 196608 | tf_op jit(solution)/shard_map/all_to_all | solution.py:29
  278.8 7.3 %fusion.23 = f32[1024,1408]{1,0:T(8,128)} fusion(bf16[768,1408]{0,1:T(8,128)(2,1)S(1)} %bitcast.39, f32[1024,768]{1,0:T(8,128)} %fusion.24, f32[768]{0:T(1024)S(1)} %copy-done.9), kind=kOutput, calls=%fused_computation.42 | convolution fusion | flops 2222456832 | bytes 11078656 | tf_op jit(solution)/shard_map/dot_general | solution.py:120
  286.1 0.6 all-to-all-done.4
  286.8 0.6 broadcast_multiply_fusion.1
  287.4 103.6 %all-reduce.2.cloned.1.call-done = f32[1081344]{0:T(1024)} async-done(((f32[1081344]{0:T(1024)}), f32[1081344]{0:T(1024)}) %all-reduce.2.cloned.1.call-update) | async-done | bytes 4325392 | tf_op jit(solution)/shard_map/psum | solution.py:52
  391.0 4.7 slice_multiply_fusion
  395.7 2.6 mul.152
  398.3 1.9 copy.31
  400.2 3.1 mul.150
  403.3 19.7 %reduce-scatter.8.cloned.1.call-done = f32[1,128,1408]{2,1,0:T(8,128)} async-done(((f32[2,128,1408]{2,1,0:T(8,128)}), f32[1,128,1408]{2,1,0:T(8,128)}) %reduce-scatter.8.cloned.1.call-update) | async-done | bytes 720912 | tf_op jit(solution)/shard_map/reduce_scatter | solution.py:66
  423.0 1.2 reduce_sum.99
  424.2 1.4 fusion.19
  425.7 24.2 %psum.43 = f32[2,1408]{1,0:T(2,128)S(1)} all-reduce(f32[2,1408]{1,0:T(2,128)S(1)} %pad_maximum_fusion.1), channel_id=1, replica_groups=mesh['dp_0'=8,'dp_1'=2,'row_0'=2,'row_1'=4,'col'=2] {'dp_0'}, use_global_device_ids=true, to_apply=%region_14.0 | all-reduce | flops 2816 | bytes 22528 | tf_op jit(solution)/shard_map/psum | solution.py:76
  449.8 10.0 %psum.44 = f32[2,1408]{1,0:T(2,128)S(1)} all-reduce(f32[2,1408]{1,0:T(2,128)S(1)} %psum.43), channel_id=1, replica_groups=mesh['dp_0'=8,'dp_1'=2,'row_0'=2,'row_1'=4,'col'=2] {'dp_1'}, use_global_device_ids=true, to_apply=%region_15.0 | all-reduce | flops 2816 | bytes 22528 | tf_op jit(solution)/shard_map/psum | solution.py:76
  459.8 7.1 %psum.45 = f32[2,1408]{1,0:T(2,128)S(1)} all-reduce(f32[2,1408]{1,0:T(2,128)S(1)} %psum.44), channel_id=1, replica_groups=mesh['dp_0'=8,'dp_1'=2,'row_0'=2,'row_1'=4,'col'=2] {'row_0'}, use_global_device_ids=true, to_apply=%region_16.0 | all-reduce | flops 2816 | bytes 22528 | tf_op jit(solution)/shard_map/psum | solution.py:76
  466.9 34.4 %psum.46 = f32[2,1408]{1,0:T(2,128)S(1)} all-reduce(f32[2,1408]{1,0:T(2,128)S(1)} %psum.45), channel_id=1, replica_groups=mesh['dp_0'=8,'dp_1'=2,'row_0'=2,'row_1'=4,'col'=2] {'row_1'}, use_global_device_ids=true, to_apply=%region_17.0 | all-reduce | flops 2816 | bytes 22528 | tf_op jit(solution)/shard_map/psum | solution.py:76
  501.3 7.2 %psum.47 = f32[2,1408]{1,0:T(2,128)S(1)} all-reduce(f32[2,1408]{1,0:T(2,128)S(1)} %psum.46), channel_id=1, replica_groups=mesh['dp_0'=8,'dp_1'=2,'row_0'=2,'row_1'=4,'col'=2] {'col'}, use_global_device_ids=true, to_apply=%region_18.0 | all-reduce | flops 2816 | bytes 22528 | tf_op jit(solution)/shard_map/psum | solution.py:76
  508.6 0.6 broadcast_multiply_fusion
  509.2 2.8 fusion.18
  (41 shorter events, 0.5 us)
Async XLA Ops:
  7.2 68.1 %all-gather.3.cloned.1.call-start = ((), (), s32[]{:S(2)}) async-start(), calls=%async_computation.8 | async-start | bytes 3244032 | tf_op jit(solution)/shard_map/all_gather | solution.py:115
  11.6 110.5 %all-gather.5.cloned.1.call-start = ((), (), s32[]{:S(2)}) async-start(), calls=%async_computation.10 | async-start | bytes 3244032 | tf_op jit(solution)/shard_map/all_gather | solution.py:126
  12.4 43.9 %copy-start.5 = (bf16[768,704]{0,1:T(8,128)(2,1)S(1)}, bf16[768,704]{0,1:T(8,128)(2,1)}, u32[]{:S(2)}) copy-start(bf16[768,704]{0,1:T(8,128)(2,1)} %param.13) | copy-start | bytes 3244036
  57.8 36.0 %all-to-all-start.1 = ((bf16[2,768,704]{1,2,0:T(8,128)(2,1)}), bf16[2,768,704]{1,2,0:T(8,128)(2,1)S(1)}, u32[]{:S(2)}, u32[]{:S(2)}) async-start(bf16[2,768,704]{1,2,0:T(8,128)(2,1)} %broadcast_in_dim.7), calls=%async_computation.1 | async-start | bytes 4325376 | tf_op jit(solution)/shard_map/all_to_all | solution.py:29
  75.3 46.9 %copy-start.9 = (f32[768]{0:T(1024)S(1)}, f32[768]{0:T(1024)}, u32[]{:S(2)}) copy-start(f32[768]{0:T(1024)} %param.12) | copy-start | bytes 9220
  93.8 35.3 %copy-start.1 = (bf16[2,768,704]{1,2,0:T(8,128)(2,1)}, bf16[2,768,704]{1,2,0:T(8,128)(2,1)S(1)}, u32[]{:S(2)}) copy-start(bf16[2,768,704]{1,2,0:T(8,128)(2,1)S(1)} %all-to-all-done.1) | copy-start | bytes 6488068
  122.1 7.0 %copy-start.8 = (bf16[1024,1408]{1,0:T(8,128)(2,1)S(1)}, bf16[1024,1408]{1,0:T(8,128)(2,1)}, u32[]{:S(2)}) copy-start(bf16[1024,1408]{1,0:T(8,128)(2,1)} %all-gather.3.cloned.1.call-done) | copy-start | bytes 8650756
  129.1 4.5 copy-start.10
  133.6 49.5 %all-to-all-start.2 = ((f32[2,704,768]{2,1,0:T(8,128)}), f32[2,704,768]{2,1,0:T(8,128)}, u32[]{:S(2)}, u32[]{:S(2)}) async-start(f32[2,704,768]{2,1,0:T(8,128)} %bitcast.37), calls=%async_computation.5 | async-start | bytes 8650752 | tf_op jit(solution)/shard_map/all_to_all | solution.py:44
  183.2 8.6 %copy-start.3 = (bf16[2,704,768]{2,1,0:T(8,128)(2,1)S(1)}, bf16[2,704,768]{2,1,0:T(8,128)(2,1)}, u32[]{:S(2)}) copy-start(bf16[2,704,768]{2,1,0:T(8,128)(2,1)} %all_to_all.26) | copy-start | bytes 6488068
  183.2 51.4 %all-to-all-start.3 = ((f32[2,768,704]{1,2,0:T(8,128)}), f32[2,768,704]{1,2,0:T(8,128)}, u32[]{:S(2)}, u32[]{:S(2)}) async-start(f32[2,768,704]{1,2,0:T(8,128)} %bitcast.36), calls=%async_computation.6 | async-start | bytes 8650752 | tf_op jit(solution)/shard_map/all_to_all | solution.py:44
  191.8 75.7 %reduce-scatter.6.cloned.1.call-start = ((), (), s32[]{:S(2)}) async-start(), calls=%async_computation.11 | async-start | bytes 7208960 | tf_op jit(solution)/shard_map/reduce_scatter | solution.py:66
  198.7 192.3 %all-reduce.2.cloned.1.call-start = ((), (), s32[]{:S(2)}) async-start(), calls=%async_computation.13 | async-start | bytes 8650752 | tf_op jit(solution)/shard_map/psum | solution.py:52
  247.5 31.2 %copy-start.2 = (bf16[2,768,704]{1,2,0:T(8,128)(2,1)S(1)}, bf16[2,768,704]{1,2,0:T(8,128)(2,1)}, u32[]{:S(2)}) copy-start(bf16[2,768,704]{1,2,0:T(8,128)(2,1)} %copy-done.1) | copy-start | bytes 6488068
  247.6 175.4 %reduce-scatter.8.cloned.1.call-start = ((), (), s32[]{:S(2)}) async-start(), calls=%async_computation.12 | async-start | bytes 2162688 | tf_op jit(solution)/shard_map/reduce_scatter | solution.py:66
  268.2 18.5 %all-to-all-start.4 = ((f32[32,1,768]{2,1,0:T(1,128)}), f32[32,1,768]{2,1,0:T(1,128)S(1)}, u32[]{:S(2)}, u32[]{:S(2)}) async-start(f32[32,1,768]{2,1,0:T(1,128)} %broadcast_in_dim.8), calls=%async_computation.7 | async-start | bytes 196608 | tf_op jit(solution)/shard_map/all_to_all | solution.py:29
  278.7 230.5 %reduce-scatter.4.cloned.1.call-start = ((), (), s32[]{:S(2)}) async-start(), calls=%async_computation.9 | async-start | bytes 6488064 | tf_op jit(solution)/shard_map/reduce_scatter | solution.py:119
  400.2 24.0 %copy-start = (bf16[128,1408]{1,0:T(8,128)(2,1)S(1)}, bf16[128,1408]{1,0:T(8,128)(2,1)}, u32[]{:S(2)}) copy-start(bf16[128,1408]{1,0:T(8,128)(2,1)} %param.8) | copy-start | bytes 1081348
  400.2 24.0 %copy-start.6 = (f32[1408]{0:T(1024)S(1)}, f32[1408]{0:T(1024)}, u32[]{:S(2)}) copy-start(f32[1408]{0:T(1024)} %param.9) | copy-start | bytes 16900
  400.2 109.0 %copy-start.4 = (bf16[128,1408]{1,0:T(8,128)(2,1)S(1)}, bf16[128,1408]{1,0:T(8,128)(2,1)}, u32[]{:S(2)}) copy-start(bf16[128,1408]{1,0:T(8,128)(2,1)} %param.15) | copy-start | bytes 1081348
  400.2 109.0 %copy-start.7 = (f32[1408]{0:T(1024)S(1)}, f32[1408]{0:T(1024)}, u32[]{:S(2)}) copy-start(f32[1408]{0:T(1024)} %param.14) | copy-start | bytes 16900
Sparse Core Ops, SparseCore 0:
  11.7 63.4 all-gather.2
  77.1 45.0 all-gather.4
  198.8 68.6 reduce-scatter.5
  269.7 121.2 all-reduce.1
  393.4 29.5 reduce-scatter.7
  425.4 72.0 reduce-scatter.3
where the time goes:
time: 525 us; the launch traced here: 519 us
  waiting for transfers between devices  263 us (50%)
  blocking collectives  125 us (24%)
  matrix products  37.1 us (7%)
  starting transfers between devices  32.4 us (6%)
  other arithmetic  26.9 us (5%)
  local copies, waits for them, and re-layouts  20.2 us (4%)
  between operations  14.2 us (3%)
    psum x1, waiting for transfers between devices, packed_total(): total = lax.psum(jnp.concatenate([a.ravel() for a in arrays]), axis)  104 us
    psum x5, blocking collectives, over_axes(): return functools.reduce(lax.psum, axes, array)  82.9 us
    all_to_all x2, waiting for transfers between devices, sum_at_owner(): tiles = lax.all_to_all(cut_along(array, dim, peers), axis, 0, 0, tiled=True)  67.7 us
    all_to_all x1, blocking collectives, from_everyone(): return lax.all_to_all(copies, axis, split_axis=0, concat_axis=0, tiled=True)  42.4 us
    reduce_scatter x2, waiting for transfers between devices, own_block(): tiles = lax.psum_scatter(tiles, axes[k], scatter_dimension=0, tiled=True)  39.6 us
    all_gather x1, waiting for transfers between devices, on_device(): upstream = lax.all_gather(cotangent, ROW, axis=0, tiled=True)  28.3 us
    all_to_all x2, starting transfers between devices, from_everyone(): return lax.all_to_all(copies, axis, split_axis=0, concat_axis=0, tiled=True)  17.8 us
    all_to_all x2, starting transfers between devices, sum_at_owner(): tiles = lax.all_to_all(cut_along(array, dim, peers), axis, 0, 0, tiled=True)  14.4 us
  transfers between devices with their start and end apart: 10, of which 9 were waited for; matrix products, arithmetic and copies ran while one was open for 13% of the time, Pallas kernels for 0%

commit v1 on v0

v1 whole, which is shorter than its diff:
```python
import math

import jax
import jax.numpy as jnp
from jax import lax
from jax.experimental import pallas as pl
from jax.experimental.pallas import tpu as pltpu
from jax.sharding import Mesh
from jax.sharding import PartitionSpec as P

MESH = pl.DeviceIdType.MESH
ROW = ("row_0", "row_1")
DP_ROW_COL = ("dp_0", "dp_1", "row_0", "row_1", "col")

EPSILON = 1e-06
GELU_ROOT = 0.7978845608028654
GELU_CUBIC = 0.044715

D = 1408
HALF = 704
QUARTER = 352
HID = 768
TOK = 128
GROUP = 1024
CHUNK_ROWS, CHUNK_COLS, FIRST = 176, 384, 96
BF = jnp.bfloat16
F32 = jnp.float32


def aligned(value, tile):
    return pl.multiple_of(value, tile)


def step_kernel(
    patches, cotangent, gain, bias, up_bias, down_bias, up, down,
    out_proj, out_back, out_mine, out_other, out_small,
    normed, cot, up_all, down_all, bias_all, gelu_d, act, slope,
    part_out, part_back, core_out, core_back, far_out, far_back, near_out, near_back,
    grad_up, grad_down, far_up, far_down, own_up, near_a, near_b,
    zsum, z_far_a, z_far_b, z_near_a, z_near_b, mine, other,
    proj, back, bias_sum, small, small_core, small_y, small_x, small_z, small_total,
    send_sems, recv_sems, local_sems,
):
    z, c = lax.axis_index("dp_0"), lax.axis_index("dp_1")
    xl, y, xh = lax.axis_index("row_0"), lax.axis_index("row_1"), lax.axis_index("col")
    x = xh * 2 + xl
    owner = xl == c

    def x_dev(d, swap=False):
        there = lax.rem(x + d, 4)
        place = {"row_0": lax.rem(there, 2), "col": lax.div(there, 2)}
        return {**place, "dp_1": 1 - c} if swap else place

    def y_dev(d):
        return {"row_1": lax.rem(y + d, 4)}

    def z_dev(d):
        return {"dp_0": lax.rem(z + d, 8)}

    partner = {"dp_1": 1 - c}
    peers = [partner]
    peers += [x_dev(d) for d in (1, 2, 3)] + [x_dev(d, True) for d in (1, 3)]
    peers += [y_dev(d) for d in (1, 2, 3)] + [z_dev(d) for d in range(1, 8)]
    barrier = pltpu.get_barrier_semaphore()
    for peer in peers:
        pl.semaphore_signal(barrier, inc=1, device_id=peer, device_id_type=MESH)
    pl.semaphore_wait(barrier, len(peers))

    count = [0]

    class Link:
        def __init__(self, src, dst, device):
            self.k = count[0]
            count[0] += 1
            self.copy = pltpu.make_async_remote_copy(
                src_ref=src, dst_ref=dst, send_sem=send_sems.at[self.k], recv_sem=recv_sems.at[self.k],
                device_id=device, device_id_type=MESH,
            )

        def start(self):
            self.copy.start()
            return self

        def sent(self):
            self.copy.wait_send()

        def got(self, dst):
            pltpu.make_async_remote_copy(
                src_ref=dst, dst_ref=dst, send_sem=send_sems.at[self.k], recv_sem=recv_sems.at[self.k],
                device_id=partner, device_id_type=MESH,
            ).wait_recv()

    always, when_owner, when_relay = [], [], []

    h_me = xh
    h_next = lax.div(lax.rem(x + 1, 4), 2)
    h_prev = lax.div(lax.rem(x + 3, 4), 2)

    def part(ref, h, first):
        start = aligned(h * HALF + (0 if first else QUARTER), 16)
        return ref.at[pl.ds(start, QUARTER)]

    class Gather:
        def __init__(self, block, whole):
            self.block, self.whole = block, whole
            lo, hi = block.at[0:QUARTER], block.at[QUARTER:HALF]
            self.a1 = Link(lo, part(whole, h_me, True), x_dev(1))
            self.b2 = Link(hi, part(whole, h_me, False), x_dev(3))
            self.b1 = Link(hi, part(whole, h_me, False), x_dev(1))
            self.a2 = Link(lo, part(whole, h_me, True), x_dev(3))
            self.ra = Link(part(whole, h_prev, True), part(whole, h_prev, True), x_dev(1))
            self.rb = Link(part(whole, h_next, False), part(whole, h_next, False), x_dev(3))
            when_owner.extend([self.a1, self.b2, self.b1, self.a2])
            when_relay.extend([self.ra, self.rb])

        def begin(self):
            for link in (self.a1, self.b2, self.b1, self.a2):
                link.start()

        def relay(self):
            self.a1.got(part(self.whole, h_prev, True))
            self.ra.start()
            self.b2.got(part(self.whole, h_next, False))
            self.rb.start()

        def finish(self):
            @pl.when(owner)
            def _():
                self.ra.got(part(self.whole, 1 - h_me, True))
                self.rb.got(part(self.whole, 1 - h_me, False))

            @pl.when(jnp.logical_not(owner))
            def _():
                self.b1.got(part(self.whole, h_prev, False))
                self.a2.got(part(self.whole, h_next, True))

    ups, downs = Gather(up, up_all), Gather(down, down_all)
    bias_link = Link(up_bias, bias_all, x_dev(1))
    when_owner.append(bias_link)

    @pl.when(owner)
    def _():
        bias_link.start()
        ups.begin()
        downs.begin()
        bias_all[...] = up_bias[...]

    def slot(ref, dy, core, lo=0, rows=TOK):
        there = lax.rem(y + dy, 4)
        return ref.at[pl.ds(aligned((there * 2 + core) * TOK + lo, 16), rows)]

    class Tokens:
        def __init__(self, own, whole):
            self.whole = whole
            self.next = Link(own, slot(whole, 0, c), y_dev(1)).start()
            self.prev = Link(own, slot(whole, 0, c), y_dev(3)).start()
            self.over = Link(own, slot(whole, 0, c), partner).start()
            always.extend([self.next, self.prev, self.over])

        def relay(self):
            whole = self.whole
            self.next.got(slot(whole, 3, c))
            self.far_a = Link(slot(whole, 3, c, 0, 64), slot(whole, 3, c, 0, 64), y_dev(1)).start()
            self.over_a = Link(slot(whole, 3, c), slot(whole, 3, c), partner).start()
            self.prev.got(slot(whole, 1, c))
            self.far_b = Link(slot(whole, 1, c, 64, 64), slot(whole, 1, c, 64, 64), y_dev(3)).start()
            self.over_b = Link(slot(whole, 1, c), slot(whole, 1, c), partner).start()
            always.extend([self.far_a, self.over_a, self.far_b, self.over_b])

        def finish(self):
            whole = self.whole
            self.far_a.got(slot(whole, 2, c, 0, 64))
            self.far_b.got(slot(whole, 2, c, 64, 64))
            self.over_far = Link(slot(whole, 2, c), slot(whole, 2, c), partner).start()
            always.append(self.over_far)
            self.over.got(slot(whole, 0, 1 - c))
            self.over_a.got(slot(whole, 3, 1 - c))
            self.over_b.got(slot(whole, 1, 1 - c))
            self.over_far.got(slot(whole, 2, 1 - c))

    def spread():
        wide = patches[...].astype(F32)
        centred = wide - jnp.mean(wide, axis=1, keepdims=True)
        inverse = lax.rsqrt(jnp.mean(centred * centred, axis=1, keepdims=True) + EPSILON)
        return centred * inverse, inverse

    own_rows = pl.ds(aligned((y * 2 + c) * TOK, TOK), TOK)
    normed[own_rows] = (spread()[0] * gain[...] + bias[...]).astype(BF)
    tok_n = Tokens(normed.at[own_rows], normed)
    tok_c = Tokens(cotangent, cot)
    cot[own_rows] = cotangent[...]

    @pl.when(owner)
    def _():
        rows = pl.ds(aligned(h_me * HALF, 16), HALF)
        up_all[rows] = up[...]
        down_all[rows] = down[...]

    tok_n.relay()

    @pl.when(jnp.logical_not(owner))
    def _():
        bias_link.got(bias_all)
        ups.relay()

    tok_n.finish()
    ups.finish()

    @pl.loop(0, GROUP // 256)
    def _(i):
        rows = pl.ds(aligned(i * 256, 256), 256)
        v = jnp.dot(normed[rows], up_all[...], preferred_element_type=F32) + bias_all[...]
        inner = jnp.tanh(GELU_ROOT * (v + GELU_CUBIC * v * v * v))
        act[rows] = (0.5 * v * (1.0 + inner)).astype(BF)
        gelu_d[rows] = 0.5 * (1.0 + inner) + 0.5 * v * (1.0 - inner * inner) * GELU_ROOT * (
            1.0 + 3.0 * GELU_CUBIC * v * v
        )

    tok_c.relay()

    @pl.when(jnp.logical_not(owner))
    def _():
        downs.relay()

    tok_c.finish()

    def outer(left, right, result):
        for lo, hi in ((0, 512), (512, 1024), (1024, D)):
            result[lo:hi] = lax.dot_general(
                left[:, lo:hi], right[...], (((0,), (0,)), ((), ())), preferred_element_type=F32
            ).astype(BF)

    class Reduce:
        def __init__(self, grad, far, swap):
            self.grad, self.far = grad, far
            h_far = 1 - h_me
            self.s0 = Link(part(grad, h_far, True), far.at[0], x_dev(1))
            self.s1 = Link(part(grad, h_far, False), far.at[1], x_dev(3))
            when_owner.extend([self.s0, self.s1])
            lo, hi = pl.ds(0, QUARTER), pl.ds(QUARTER, QUARTER)
            self.s2 = Link(part(grad, h_next, False), near_a.at[hi], x_dev(1, swap))
            self.s4 = Link(part(grad, h_prev, True), near_b.at[lo], x_dev(3, swap))
            self.s3 = Link(part(grad, h_next, True), near_a.at[lo], x_dev(1, swap))
            self.s5 = Link(part(grad, h_prev, False), near_b.at[hi], x_dev(3, swap))
            when_relay.extend([self.s2, self.s4, self.s3, self.s5])

        def begin(self):
            @pl.when(owner)
            def _():
                self.s0.start()
                self.s1.start()

            @pl.when(jnp.logical_not(owner))
            def _():
                self.s2.start()
                self.s4.start()

        def middle(self):
            grad, far = self.grad, self.far

            @pl.when(jnp.logical_not(owner))
            def _():
                for link, other_link, h, first, k in ((self.s0, self.s3, h_next, True, 0), (self.s1, self.s5, h_prev, False, 1)):
                    link.got(far.at[k])
                    rows = pl.ds(aligned(h * HALF + (0 if first else QUARTER), 16), QUARTER)
                    grad[rows] = (grad[rows].astype(F32) + far[k].astype(F32)).astype(BF)
                    other_link.start()

        def finish(self):
            lo, hi = pl.ds(0, QUARTER), pl.ds(QUARTER, QUARTER)
            self.s2.got(near_a.at[hi])
            self.s4.got(near_b.at[lo])
            self.s3.got(near_a.at[lo])
            self.s5.got(near_b.at[hi])

    red_down = Reduce(grad_down, far_down, False)
    red_up = Reduce(grad_up, far_up, True)
    own_rows_w = pl.ds(aligned(h_me * HALF, 16), HALF)
    own_link = Link(grad_up.at[own_rows_w], own_up, partner)
    when_owner.append(own_link)

    outer(cot, act, grad_down)
    red_down.begin()
    downs.finish()

    bias_sum[...] = jnp.zeros_like(bias_sum)

    @pl.loop(0, GROUP // 256)
    def _(i):
        rows = pl.ds(aligned(i * 256, 256), 256)
        s = jnp.dot(cot[rows], down_all[...], preferred_element_type=F32) * gelu_d[rows]
        s = s.astype(BF)
        slope[rows] = s
        bias_sum[...] += jnp.sum(s.astype(F32), axis=0, keepdims=True)

    outer(normed, slope, grad_up)
    red_up.begin()

    @pl.when(owner)
    def _():
        own_link.start()

    red_down.middle()

    def across(left, right, result):
        @pl.loop(0, GROUP // 256)
        def _(i):
            rows = pl.ds(aligned(i * 256, 256), 256)
            result[rows] = lax.dot_general(
                left[rows], right[...], (((1,), (1,)), ((), ())), preferred_element_type=F32
            ).astype(BF)

    class Scatter:
        def __init__(self, partial, core, far, near):
            self.partial, self.core, self.far, self.near = partial, core, far, near
            self.over = []
            for dy in (2, 1, 3, 0):
                there = lax.rem(y + dy, 4)
                self.over.append((dy, Link(slot(partial, dy, 1 - c), core.at[there], partner).start()))
            always.extend(link for _, link in self.over)

        def combine(self):
            partial, core = self.partial, self.core
            for dy, link in self.over:
                there = lax.rem(y + dy, 4)
                link.got(core.at[there])
                if dy == 0:
                    continue
                rows = pl.ds(aligned((there * 2 + c) * TOK, TOK), TOK)
                partial[rows] = (partial[rows].astype(F32) + core[there].astype(F32)).astype(BF)
                if dy == 2:
                    self.t0 = Link(slot(partial, 2, c, 0, 64), self.far.at[0], y_dev(1)).start()
                    self.t1 = Link(slot(partial, 2, c, 64, 64), self.far.at[1], y_dev(3)).start()
                elif dy == 1:
                    self.t2 = Link(slot(partial, 1, c, 64, 64), self.near.at[0, pl.ds(64, 64)], y_dev(1)).start()
                else:
                    self.t3 = Link(slot(partial, 3, c, 0, 64), self.near.at[1, pl.ds(0, 64)], y_dev(3)).start()
            always.extend([self.t0, self.t1, self.t2, self.t3])

        def middle(self):
            partial, far = self.partial, self.far
            for dy, lo, k, link in ((1, 0, 0, self.t0), (3, 64, 1, self.t1)):
                link.got(far.at[k])
                there = lax.rem(y + dy, 4)
                rows = pl.ds(aligned((there * 2 + c) * TOK + lo, 16), 64)
                partial[rows] = (partial[rows].astype(F32) + far[k].astype(F32)).astype(BF)
                onward = Link(slot(partial, dy, c, lo, 64), self.near.at[k, pl.ds(lo, 64)], y_dev(dy)).start()
                always.append(onward)
                if k == 0:
                    self.t4 = onward
                else:
                    self.t5 = onward

        def finish(self):
            near = self.near
            self.t2.got(near.at[0, pl.ds(64, 64)])
            self.t3.got(near.at[1, pl.ds(0, 64)])
            self.t4.got(near.at[0, pl.ds(0, 64)])
            self.t5.got(near.at[1, pl.ds(64, 64)])
            own = self.partial[own_rows].astype(F32) + self.core[y].astype(F32)
            return own + near[0].astype(F32) + near[1].astype(F32)

    across(slope, up_all, part_back)
    sc_back = Scatter(part_back, core_back, far_back, near_back)
    across(act, down_all, part_out)
    sc_out = Scatter(part_out, core_out, far_out, near_out)
    sc_back.combine()
    sc_out.combine()
    red_up.middle()
    sc_back.middle()
    sc_out.middle()

    back[...] = sc_back.finish()
    standard, inverse = spread()
    nb = back[...]
    rows_small = (
        (0, D // 128, jnp.sum(nb * standard, axis=0, keepdims=True)),
        (D // 128, D // 128, jnp.sum(nb, axis=0, keepdims=True)),
        (2 * (D // 128), HID // 128, bias_sum[...]),
    )
    small[...] = jnp.zeros_like(small)
    for first, length, row in rows_small:
        for i in range(length):
            small[first + i : first + i + 1, :] = row[:, 128 * i : 128 * (i + 1)]
    n_norm = 2 * (D // 128)
    small_over = Link(small, small_core, partner).start()
    always.append(small_over)
    scaled = nb * gain[...]
    back[...] = inverse * (
        scaled
        - jnp.mean(scaled, axis=1, keepdims=True)
        - standard * jnp.mean(scaled * standard, axis=1, keepdims=True)
    )
    put_back = pltpu.make_async_copy(back, out_back, local_sems.at[0])
    put_back.start()

    def load_own(source):
        for k in range(8):
            r = slice((k % 4) * CHUNK_ROWS, (k % 4 + 1) * CHUNK_ROWS)
            l = slice((k // 4) * CHUNK_COLS, (k // 4 + 1) * CHUNK_COLS)
            zsum[k] = (
                source(k).astype(F32) + near_a[r, l].astype(F32) + near_b[r, l].astype(F32)
            ).astype(BF)

    @pl.when(owner)
    def _():
        red_down.finish()

        def source(k):
            rows = pl.ds(aligned(h_me * HALF + (k % 4) * CHUNK_ROWS, 16), CHUNK_ROWS)
            return grad_down[rows, (k // 4) * CHUNK_COLS : (k // 4 + 1) * CHUNK_COLS]

        load_own(source)

    @pl.when(jnp.logical_not(owner))
    def _():
        own_link.got(own_up)
        red_up.finish()

        def source(k):
            return own_up[
                (k % 4) * CHUNK_ROWS : (k % 4 + 1) * CHUNK_ROWS, (k // 4) * CHUNK_COLS : (k // 4 + 1) * CHUNK_COLS
            ]

        load_own(source)

    def at_z(d):
        return lax.rem(z + d, 8)

    head, tail = pl.ds(0, FIRST), pl.ds(FIRST, CHUNK_ROWS - FIRST)
    f0 = Link(zsum.at[at_z(4), head], z_far_a, z_dev(1)).start()
    b0 = Link(zsum.at[at_z(4), tail], z_far_b, z_dev(7)).start()
    always.extend([f0, b0])

    def add_rows(k, rows, incoming):
        zsum[k, rows] = (zsum[k, rows].astype(F32) + incoming.astype(F32)).astype(BF)

    small_over.got(small_core)
    keep = lax.broadcasted_iota(jnp.int32, small.shape, 0) < n_norm
    small_y[y] = small[...] + jnp.where(keep, small_core[...], 0.0)
    y_links = [Link(small_y.at[y], small_y.at[y], y_dev(d)).start() for d in (1, 2, 3)]
    always.extend(y_links)

    f0.got(z_far_a)
    add_rows(at_z(3), head, z_far_a[...])
    f1 = Link(zsum.at[at_z(3)], z_near_a.at[0], z_dev(1)).start()
    b0.got(z_far_b)
    add_rows(at_z(5), tail, z_far_b[...])
    b1 = Link(zsum.at[at_z(5)], z_near_b.at[0], z_dev(7)).start()
    always.extend([f1, b1])

    for d, link in zip((1, 2, 3), y_links):
        link.got(small_y.at[lax.rem(y + 4 - d, 4)])
    ysum = small_y[0] + small_y[1] + small_y[2] + small_y[3]
    small_x[x] = jnp.where(keep, ysum, small[...])
    x_links = [Link(small_x.at[x], small_x.at[x], x_dev(d)).start() for d in (1, 2, 3)]
    always.extend(x_links)

    everything = pl.ds(0, CHUNK_ROWS)
    f1.got(z_near_a.at[0])
    add_rows(at_z(2), everything, z_near_a[0])
    f2 = Link(zsum.at[at_z(2)], z_near_a.at[1], z_dev(1)).start()
    b1.got(z_near_b.at[0])
    add_rows(at_z(6), everything, z_near_b[0])
    b2 = Link(zsum.at[at_z(6)], z_near_b.at[1], z_dev(7)).start()
    always.extend([f2, b2])

    for d, link in zip((1, 2, 3), x_links):
        link.got(small_x.at[lax.rem(x + 4 - d, 4)])
    small_z[z] = small_x[0] + small_x[1] + small_x[2] + small_x[3]
    z_links = [Link(small_z.at[z], small_z.at[z], z_dev(d)).start() for d in range(1, 8)]
    always.extend(z_links)

    f2.got(z_near_a.at[1])
    add_rows(at_z(1), everything, z_near_a[1])
    f3 = Link(zsum.at[at_z(1)], z_near_a.at[2], z_dev(1)).start()
    b2.got(z_near_b.at[1])
    add_rows(at_z(7), everything, z_near_b[1])
    b3 = Link(zsum.at[at_z(7)], z_near_b.at[2], z_dev(7)).start()
    always.extend([f3, b3])

    for d, link in zip(range(1, 8), z_links):
        link.got(small_z.at[at_z(8 - d)])
    total = small_z[0]
    for k in range(1, 8):
        total = total + small_z[k]
    small_total[0] = total
    last_over = Link(small_total.at[0], small_total.at[1], partner).start()
    always.append(last_over)

    f3.got(z_near_a.at[2])
    b3.got(z_near_b.at[2])
    mine[z] = (zsum[z].astype(F32) + z_near_a[2].astype(F32) + z_near_b[2].astype(F32)).astype(BF)

    def forward(k, device):
        link = Link(mine.at[k], mine.at[k], device).start()
        always.append(link)
        return link

    overs = []

    def hand_over(k):
        link = Link(mine.at[k], other.at[k], partner).start()
        always.append(link)
        overs.append((link, k))

    ga = forward(z, z_dev(1))
    gb = forward(z, z_dev(7))
    hand_over(z)
    for d in (1, 2):
        ga.got(mine.at[at_z(8 - d)])
        ga = forward(at_z(8 - d), z_dev(1))
        hand_over(at_z(8 - d))
        gb.got(mine.at[at_z(d)])
        gb = forward(at_z(d), z_dev(7))
        hand_over(at_z(d))
    ga.got(mine.at[at_z(5)])
    ha = Link(mine.at[at_z(5), head], mine.at[at_z(5), head], z_dev(1)).start()
    hand_over(at_z(5))
    gb.got(mine.at[at_z(3)])
    hb = Link(mine.at[at_z(3), tail], mine.at[at_z(3), tail], z_dev(7)).start()
    hand_over(at_z(3))
    always.extend([ha, hb])

    proj[...] = sc_out.finish() + down_bias[...]
    put_proj = pltpu.make_async_copy(proj, out_proj, local_sems.at[1])
    put_proj.start()

    ha.got(mine.at[at_z(4), head])
    hb.got(mine.at[at_z(4), tail])
    hand_over(at_z(4))
    put_mine = pltpu.make_async_copy(mine, out_mine, local_sems.at[2])
    put_mine.start()
    for link, k in overs:
        link.got(other.at[k])
    put_other = pltpu.make_async_copy(other, out_other, local_sems.at[3])
    put_other.start()
    last_over.got(small_total.at[1])
    put_small = pltpu.make_async_copy(small_total, out_small, local_sems.at[4])
    put_small.start()

    for link in always:
        link.sent()

    @pl.when(owner)
    def _():
        for link in when_owner:
            link.sent()

    @pl.when(jnp.logical_not(owner))
    def _():
        for link in when_relay:
            link.sent()

    for put in (put_back, put_proj, put_mine, put_other, put_small):
        put.wait()
    assert count[0] <= N_LINKS


N_LINKS = 128


def on_device(patches, norm_gain, norm_bias, up_weight, up_bias, down_weight, down_bias, cotangent):
    scaling = 1.0 / math.sqrt(TOK * 256)
    vmem = pl.BlockSpec(memory_space=pltpu.VMEM)
    hbm = pl.BlockSpec(memory_space=pl.ANY)

    def V(*shape, dtype=BF):
        return pltpu.VMEM(shape, dtype)

    proj, back, mine, other, small = pl.pallas_call(
        step_kernel,
        out_shape=(
            jax.ShapeDtypeStruct((TOK, D), F32),
            jax.ShapeDtypeStruct((TOK, D), F32),
            jax.ShapeDtypeStruct((8, CHUNK_ROWS, CHUNK_COLS), BF),
            jax.ShapeDtypeStruct((8, CHUNK_ROWS, CHUNK_COLS), BF),
            jax.ShapeDtypeStruct((2, 32, 128), F32),
        ),
        in_specs=[vmem] * 8,
        out_specs=[hbm] * 5,
        scratch_shapes=[
            V(GROUP, D), V(GROUP, D), V(D, HID), V(D, HID), V(1, HID, dtype=F32),
            V(GROUP, HID, dtype=F32), V(GROUP, HID), V(GROUP, HID),
            V(GROUP, D), V(GROUP, D), V(4, TOK, D), V(4, TOK, D),
            V(2, 64, D), V(2, 64, D), V(2, TOK, D), V(2, TOK, D),
            V(D, HID), V(D, HID), V(2, QUARTER, HID), V(2, QUARTER, HID), V(HALF, HID),
            V(HALF, HID), V(HALF, HID),
            V(8, CHUNK_ROWS, CHUNK_COLS), V(FIRST, CHUNK_COLS), V(CHUNK_ROWS - FIRST, CHUNK_COLS),
            V(3, CHUNK_ROWS, CHUNK_COLS), V(3, CHUNK_ROWS, CHUNK_COLS),
            V(8, CHUNK_ROWS, CHUNK_COLS), V(8, CHUNK_ROWS, CHUNK_COLS),
            V(TOK, D, dtype=F32), V(TOK, D, dtype=F32), V(1, HID, dtype=F32),
            V(32, 128, dtype=F32), V(32, 128, dtype=F32), V(4, 32, 128, dtype=F32),
            V(4, 32, 128, dtype=F32), V(8, 32, 128, dtype=F32), V(2, 32, 128, dtype=F32),
            pltpu.SemaphoreType.DMA((N_LINKS,)),
            pltpu.SemaphoreType.DMA((N_LINKS,)),
            pltpu.SemaphoreType.DMA((5,)),
        ],
        compiler_params=pltpu.CompilerParams(
            collective_id=0, has_side_effects=True, vmem_limit_bytes=63 * 1024 * 1024
        ),
    )(
        patches, cotangent, norm_gain[None], norm_bias[None], up_bias[None], down_bias[None],
        up_weight, down_weight.T,
    )

    owner = lax.axis_index("row_0") == lax.axis_index("dp_1")

    def whole(chunks):
        left, right = chunks.reshape(2, HALF, CHUNK_COLS)
        return jnp.concatenate([left, right], axis=1).astype(F32) * scaling

    up_grad = whole(jnp.where(owner, other, mine))
    down_grad = whole(jnp.where(owner, mine, other)).T
    small = small * scaling
    n = D // 128
    norm_grad = small[0, : 2 * n].reshape(2, D)
    bias_grad = jnp.where(owner, small[0], small[1])[2 * n : 2 * n + HID // 128].reshape(HID)
    output = proj + patches.astype(F32)
    patch_grad = back + cotangent.astype(F32)
    return output, patch_grad, up_grad, down_grad, bias_grad, norm_grad


def solution(mesh):
    split = Mesh(
        mesh.devices.reshape(8, 2, 2, 4, mesh.shape["col"]),
        ("dp_0", "dp_1", "row_0", "row_1", "col"),
    )
    return jax.shard_map(
        on_device,
        mesh=split,
        in_specs=(
            P(DP_ROW_COL, None), P(), P(), P("col", ROW), P(ROW), P(ROW, "col"), P(), P(DP_ROW_COL, None),
        ),
        out_specs=(
            P(DP_ROW_COL, None), P(DP_ROW_COL, None), P("col", ROW), P(ROW, "col"), P(ROW), P(),
        ),
        check_vma=False,
    )
```

time: 525 us -> 148 us (0.28); the launches traced: 519 us -> 148 us
  waiting for transfers between devices: 263 us -> 0 us
  Pallas kernels: 0 us -> 135 us
  blocking collectives: 125 us -> 0 us
  matrix products: 37.1 us -> 0 us
  starting transfers between devices: 32.4 us -> 0 us
  other arithmetic: 26.9 us -> 6.57 us
  local copies, waits for them, and re-layouts: 20.2 us -> 6.01 us
  between operations: 14.2 us -> 0.72 us
    pallas_call x0 -> x1, Pallas kernels: none -> 135 us  [on_device(): pl.pallas_call(step_kernel, out_shape=(jax.ShapeDtypeStruct((TOK, D), F32...]
    psum x1 -> x0, waiting for transfers between devices: 104 us -> none  [packed_total(): total = lax.psum(jnp.concatenate([a.ravel() for a in arrays]), axis)]
    psum x5 -> x0, blocking collectives: 82.9 us -> none  [over_axes(): return functools.reduce(lax.psum, axes, array)]
    all_to_all x4 -> x0, waiting for transfers between devices: 80.1 us -> none  [the longest x2 67.7 us: sum_at_owner(): tiles = lax.all_to_all(cut_along(array, dim, peers), axis, 0, 0, tiled=True)]
    all_to_all x1 -> x0, blocking collectives: 42.4 us -> none  [from_everyone(): return lax.all_to_all(copies, axis, split_axis=0, concat_axis=0, tiled=True)]
    reduce_scatter x3 -> x0, waiting for transfers between devices: 39.6 us -> none  [the longest x2 39.6 us: own_block(): tiles = lax.psum_scatter(tiles, axes[k], scatter_dimension=0, tiled=True)]
    all_gather x2 -> x0, waiting for transfers between devices: 38.5 us -> none  [the longest x1 28.3 us: on_device(): upstream = lax.all_gather(cotangent, ROW, axis=0, tiled=True)]
    dot_general x6 -> x0, matrix products: 37.1 us -> none  [the longest x2 12.1 us: contract_rows(): lax.dot_general(left, right, (((0,), (0,)), ((), ())), preferred_element_...]
  transfers between devices with their start and end apart: 10 -> 0, of which waited for: 9 -> 0; matrix products, arithmetic and copies ran while one was open for 13% -> 0% of each run, Pallas kernels for 0% -> 0%
where the time goes in v1:
time: 148 us
  Pallas kernels  135 us (91%)
  other arithmetic  6.57 us (4%)
  local copies, waits for them, and re-layouts  6.01 us (4%)
    pallas_call x1, Pallas kernels, on_device(): pl.pallas_call(step_kernel, out_shape=(jax.ShapeDtypeStruct((TOK, D), F32...  135 us

profile of v1, /device:TPU:7, one launch (start us, length us, event | category | flops | bytes accessed | tf_op | source)
XLA Modules:
  0.0 147.9 jit_solution(10609388997923183274)
XLA Ops:
  0.6 1.3 broadcast_in_dim.14.up_bias
  1.9 1.3 broadcast_in_dim.12.gain
  3.2 1.3 broadcast_in_dim.13.bias
  4.5 1.3 broadcast_in_dim.15.down_bias
  5.8 0.0 copy-start
  5.8 0.0 copy-start.1
  5.8 134.7 %shard_map.127 = (f32[128,1408]{1,0:T(8,128)}, f32[128,1408]{1,0:T(8,128)}, bf16[8,176,384]{2,1,0:T(8,128)(2,1)}, bf16[8,176,384]{2,1,0:T(8,128)(2,1)}, f32[2,32,128]{2,1,0:T(8,128)}) custom-call(bf16[128,1408]{1,0:T(8,128)(2,1)} %patches.1, bf16[128,1408]{1,0:T(8,128)(2,1)} %cotangent.1, f32[1,1408]{1,0:T(1,128)} %broadcast_in_dim.12.gain, ...), custom_call_target="tpu_custom_call" | custom-call | tf_op jit(solution)/shard_map/pallas_call | solution.py:571
  140.5 0.0 copy-done
  140.5 0.0 copy-done.1
  140.5 0.0 copy-start.4
  140.5 0.0 copy-start.2
  140.5 0.0 copy-start.3
  140.5 2.7 %convert_add_fusion = (f32[128,1408]{1,0:T(8,128)}, f32[128,1408]{1,0:T(8,128)}) fusion(f32[128,1408]{1,0:T(8,128)} %get-tuple-element.12, bf16[128,1408]{1,0:T(8,128)(2,1)S(1)} %copy-done.1, f32[128,1408]{1,0:T(8,128)} %get-tuple-element.11, bf16[128,1408]{1,0:T(8,128)(2,1)S(1)} %copy-done), kind=kLoop, calls=%fused_computation.4 | loop fusion | flops 720896 | bytes 3604480 | tf_op jit(solution)/shard_map/add | solution.py:620
  143.2 0.0 copy-done.4
  143.2 0.6 reshape_squeeze.3
  143.8 0.6 fusion
  144.4 0.0 copy-done.2
  144.4 0.0 copy-done.3
  144.4 0.2 broadcast_select_fusion
  144.6 0.2 fusion.1
  144.9 1.5 %multiply_bitcast_fusion = f32[768,704]{0,1:T(8,128)} fusion(bf16[704,384]{1,0:T(8,128)(2,1)S(1)} %bitcast.12, bf16[704,384]{1,0:T(8,128)(2,1)S(1)} %bitcast.11), kind=kLoop, calls=%fused_computation | loop fusion | flops 2703360 | bytes 3244032 | tf_op jit(solution)/shard_map/transpose | solution.py:614
  146.4 1.5 %convert_multiply_fusion = f32[704,768]{1,0:T(8,128)} fusion(bf16[704,384]{1,0:T(8,128)(2,1)S(1)} %bitcast.9, bf16[704,384]{1,0:T(8,128)(2,1)S(1)} %bitcast.10), kind=kLoop, calls=%fused_computation.1 | loop fusion | flops 2703360 | bytes 3244032 | tf_op jit(solution)/shard_map/mul | solution.py:611
  (3 shorter events, 0.0 us)
Async XLA Ops:
  5.8 134.7 %copy-start = (bf16[128,1408]{1,0:T(8,128)(2,1)S(1)}, bf16[128,1408]{1,0:T(8,128)(2,1)}, u32[]{:S(2)}) copy-start(bf16[128,1408]{1,0:T(8,128)(2,1)} %patches.1) | copy-start | bytes 1081348
  5.8 134.7 %copy-start.1 = (bf16[128,1408]{1,0:T(8,128)(2,1)S(1)}, bf16[128,1408]{1,0:T(8,128)(2,1)}, u32[]{:S(2)}) copy-start(bf16[128,1408]{1,0:T(8,128)(2,1)} %cotangent.1) | copy-start | bytes 1081348
  140.5 2.7 %copy-start.4 = (f32[2,32,128]{2,1,0:T(8,128)S(1)}, f32[2,32,128]{2,1,0:T(8,128)}, u32[]{:S(2)}) copy-start(f32[2,32,128]{2,1,0:T(8,128)} %get-tuple-element.15) | copy-start | bytes 98308
  140.5 4.0 %copy-start.2 = (bf16[8,176,384]{2,1,0:T(8,128)(2,1)S(1)}, bf16[8,176,384]{2,1,0:T(8,128)(2,1)}, u32[]{:S(2)}) copy-start(bf16[8,176,384]{2,1,0:T(8,128)(2,1)} %get-tuple-element.14) | copy-start | bytes 3244036
  140.5 3.9 %copy-start.3 = (bf16[8,176,384]{2,1,0:T(8,128)(2,1)S(1)}, bf16[8,176,384]{2,1,0:T(8,128)(2,1)}, u32[]{:S(2)}) copy-start(bf16[8,176,384]{2,1,0:T(8,128)(2,1)} %get-tuple-element.13) | copy-start | bytes 3244036

commit v2 on v1

v2 whole, which is shorter than its diff:
```python
import math

import jax
import jax.numpy as jnp
from jax import lax
from jax.experimental import pallas as pl
from jax.experimental.pallas import tpu as pltpu
from jax.sharding import Mesh
from jax.sharding import PartitionSpec as P

MESH = pl.DeviceIdType.MESH
ROW = ("row_0", "row_1")
DP_ROW_COL = ("dp_0", "dp_1", "row_0", "row_1", "col")

EPSILON = 1e-06
GELU_ROOT = 0.7978845608028654
GELU_CUBIC = 0.044715

D = 1408
HALF = 704
QUARTER = 352
HID = 768
TOK = 128
GROUP = 1024
CHUNK_ROWS, CHUNK_COLS = 176, 384
UNITS = (pl.ds(0, 96), pl.ds(96, 80))
BF = jnp.bfloat16
F32 = jnp.float32


def aligned(value, tile):
    return pl.multiple_of(value, tile)


def step_kernel(
    patches_in, cotangent_in, gain, bias, up_bias, down_bias, up, down,
    out_proj, out_back, out_mine, out_other, out_small,
    patches, normed, cot, up_all, down_all, bias_all, gelu_d, act, slope,
    part_out, part_back, core_out, core_back, far_out, far_back, near_out, near_back,
    grad_up, grad_down, far_up, far_down, own_up, near_a, near_b,
    zsum, z_near_a, z_near_b, mine, other,
    proj, back, bias_sum, small, small_core, small_y, small_x, small_z, small_total,
    send_sems, recv_sems, local_sems,
):
    z, c = lax.axis_index("dp_0"), lax.axis_index("dp_1")
    xl, y, xh = lax.axis_index("row_0"), lax.axis_index("row_1"), lax.axis_index("col")
    x = xh * 2 + xl
    owner = xl == c

    def x_dev(d, swap=False):
        there = lax.rem(x + d, 4)
        place = {"row_0": lax.rem(there, 2), "col": lax.div(there, 2)}
        return {**place, "dp_1": 1 - c} if swap else place

    def y_dev(d):
        return {"row_1": lax.rem(y + d, 4)}

    def z_dev(d):
        return {"dp_0": lax.rem(z + d, 8)}

    partner = {"dp_1": 1 - c}
    peers = [partner]
    peers += [x_dev(d) for d in (1, 2, 3)] + [x_dev(d, True) for d in (1, 3)]
    peers += [y_dev(d) for d in (1, 2, 3)] + [z_dev(d) for d in range(1, 8)]
    own_rows = pl.ds(aligned((y * 2 + c) * TOK, TOK), TOK)
    own_block = pl.ds(aligned(xh * HALF, 16), HALF)
    load_patches = pltpu.make_async_copy(patches_in, patches, local_sems.at[5])
    load_cot = pltpu.make_async_copy(cotangent_in, cot.at[own_rows], local_sems.at[6])
    load_up = pltpu.make_async_copy(up, up_all.at[own_block], local_sems.at[7])
    load_down = pltpu.make_async_copy(down, down_all.at[own_block], local_sems.at[8])
    load_patches.start()
    load_cot.start()

    @pl.when(owner)
    def _():
        load_up.start()
        load_down.start()

    barrier = pltpu.get_barrier_semaphore()
    for peer in peers:
        pl.semaphore_signal(barrier, inc=1, device_id=peer, device_id_type=MESH)
    pl.semaphore_wait(barrier, len(peers))

    count = [0]

    class Link:
        def __init__(self, src, dst, device):
            self.k = count[0]
            count[0] += 1
            self.copy = pltpu.make_async_remote_copy(
                src_ref=src, dst_ref=dst, send_sem=send_sems.at[self.k], recv_sem=recv_sems.at[self.k],
                device_id=device, device_id_type=MESH,
            )

        def start(self):
            self.copy.start()
            return self

        def sent(self):
            self.copy.wait_send()

        def got(self, dst):
            pltpu.make_async_remote_copy(
                src_ref=dst, dst_ref=dst, send_sem=send_sems.at[self.k], recv_sem=recv_sems.at[self.k],
                device_id=partner, device_id_type=MESH,
            ).wait_recv()

    always, when_owner, when_relay = [], [], []

    h_me = xh
    h_next = lax.div(lax.rem(x + 1, 4), 2)
    h_prev = lax.div(lax.rem(x + 3, 4), 2)

    lanes_x = pl.ds(aligned(lax.rem(z, 2) * CHUNK_COLS, 128), CHUNK_COLS)
    lanes_z = pl.ds(aligned((1 - lax.rem(z, 2)) * CHUNK_COLS, 128), CHUNK_COLS)

    def part(ref, h, first, lanes):
        start = aligned(h * HALF + (0 if first else QUARTER), 16)
        return ref.at[pl.ds(start, QUARTER), lanes]

    class Gather:
        def __init__(self, whole):
            def link(h, first, device):
                return Link(part(whole, h, first, lanes_x), part(whole, h, first, lanes_x), device)

            self.whole = whole
            self.a1, self.b2 = link(h_me, True, x_dev(1)), link(h_me, False, x_dev(3))
            self.b1, self.a2 = link(h_me, False, x_dev(1)), link(h_me, True, x_dev(3))
            self.ra, self.rb = link(h_prev, True, x_dev(1)), link(h_next, False, x_dev(3))
            self.oa, self.ob = link(1 - h_me, True, z_dev(1)), link(1 - h_me, False, z_dev(7))
            self.pa, self.nb = link(h_prev, True, z_dev(1)), link(h_next, False, z_dev(7))
            self.pb, self.na = link(h_prev, False, z_dev(7)), link(h_next, True, z_dev(1))
            when_owner.extend([self.a1, self.b2, self.b1, self.a2, self.oa, self.ob])
            when_relay.extend([self.ra, self.rb, self.pa, self.nb, self.pb, self.na])

        def here(self, h, first):
            return part(self.whole, h, first, lanes_x)

        def there(self, h, first):
            return part(self.whole, h, first, lanes_z)

        def begin(self):
            for link in (self.a1, self.b2, self.b1, self.a2):
                link.start()

        def relay(self):
            self.a1.got(self.here(h_prev, True))
            self.ra.start()
            self.pa.start()
            self.b2.got(self.here(h_next, False))
            self.rb.start()
            self.nb.start()

        def relay_last(self):
            self.b1.got(self.here(h_prev, False))
            self.pb.start()
            self.a2.got(self.here(h_next, True))
            self.na.start()

        def pass_on(self):
            self.ra.got(self.here(1 - h_me, True))
            self.oa.start()
            self.rb.got(self.here(1 - h_me, False))
            self.ob.start()

        def finish(self):
            @pl.when(owner)
            def _():
                self.oa.got(self.there(1 - h_me, True))
                self.ob.got(self.there(1 - h_me, False))

            @pl.when(jnp.logical_not(owner))
            def _():
                self.pa.got(self.there(h_prev, True))
                self.nb.got(self.there(h_next, False))
                self.pb.got(self.there(h_prev, False))
                self.na.got(self.there(h_next, True))

    ups, downs = Gather(up_all), Gather(down_all)
    bias_link = Link(up_bias, bias_all, x_dev(1))
    when_owner.append(bias_link)

    @pl.when(owner)
    def _():
        load_up.wait()
        ups.begin()
        bias_link.start()
        load_down.wait()
        downs.begin()
        bias_all[...] = up_bias[...]

    def slot(ref, dy, core, lo=0, rows=TOK):
        there = lax.rem(y + dy, 4)
        return ref.at[pl.ds(aligned((there * 2 + core) * TOK + lo, 16), rows)]

    class Tokens:
        def __init__(self, own, whole):
            self.whole = whole
            self.next = Link(own, slot(whole, 0, c), y_dev(1)).start()
            self.prev = Link(own, slot(whole, 0, c), y_dev(3)).start()
            self.over = Link(own, slot(whole, 0, c), partner).start()
            always.extend([self.next, self.prev, self.over])

        def relay(self):
            whole = self.whole
            self.next.got(slot(whole, 3, c))
            self.far_a = Link(slot(whole, 3, c, 0, 64), slot(whole, 3, c, 0, 64), y_dev(1)).start()
            self.over_a = Link(slot(whole, 3, c), slot(whole, 3, c), partner).start()
            self.prev.got(slot(whole, 1, c))
            self.far_b = Link(slot(whole, 1, c, 64, 64), slot(whole, 1, c, 64, 64), y_dev(3)).start()
            self.over_b = Link(slot(whole, 1, c), slot(whole, 1, c), partner).start()
            always.extend([self.far_a, self.over_a, self.far_b, self.over_b])

        def finish(self):
            whole = self.whole
            self.far_a.got(slot(whole, 2, c, 0, 64))
            self.far_b.got(slot(whole, 2, c, 64, 64))
            self.over_far = Link(slot(whole, 2, c), slot(whole, 2, c), partner).start()
            always.append(self.over_far)
            self.over.got(slot(whole, 0, 1 - c))
            self.over_a.got(slot(whole, 3, 1 - c))
            self.over_b.got(slot(whole, 1, 1 - c))
            self.over_far.got(slot(whole, 2, 1 - c))

    def spread():
        wide = patches[...].astype(F32)
        centred = wide - jnp.mean(wide, axis=1, keepdims=True)
        inverse = lax.rsqrt(jnp.mean(centred * centred, axis=1, keepdims=True) + EPSILON)
        return centred * inverse, inverse

    load_cot.wait()
    load_patches.wait()
    normed[own_rows] = (spread()[0] * gain[...][None] + bias[...][None]).astype(BF)
    tok_n = Tokens(normed.at[own_rows], normed)
    tok_c = Tokens(cot.at[own_rows], cot)

    @pl.when(jnp.logical_not(owner))
    def _():
        ups.relay()

    tok_n.relay()

    @pl.when(owner)
    def _():
        ups.pass_on()

    @pl.when(jnp.logical_not(owner))
    def _():
        bias_link.got(bias_all)
        ups.relay_last()
        downs.relay()

    tok_c.relay()

    @pl.when(owner)
    def _():
        downs.pass_on()

    @pl.when(jnp.logical_not(owner))
    def _():
        downs.relay_last()

    tok_n.finish()
    ups.finish()

    @pl.loop(0, GROUP // 256)
    def _(i):
        rows = pl.ds(aligned(i * 256, 256), 256)
        v = jnp.dot(normed[rows], up_all[...], preferred_element_type=F32) + bias_all[...][None]
        inner = jnp.tanh(GELU_ROOT * (v + GELU_CUBIC * v * v * v))
        act[rows] = (0.5 * v * (1.0 + inner)).astype(BF)
        gelu_d[rows] = 0.5 * (1.0 + inner) + 0.5 * v * (1.0 - inner * inner) * GELU_ROOT * (
            1.0 + 3.0 * GELU_CUBIC * v * v
        )

    tok_c.finish()

    def outer(left, right, result):
        for lo, hi in ((0, 512), (512, 1024), (1024, D)):
            block = lax.dot_general(
                left[:, lo:hi], right[...], (((0,), (0,)), ((), ())), preferred_element_type=F32
            ).astype(BF)
            while lo < hi:
                j, r = divmod(lo, CHUNK_ROWS)
                rows = min(CHUNK_ROWS - r, hi - lo)
                result[j, r : r + rows] = block[:rows]
                block, lo = block[rows:], lo + rows

    class Reduce:
        def __init__(self, grad, far, swap):
            self.grad, self.far, self.links = grad, far, []
            lo, hi = pl.ds(0, 2), pl.ds(2, 2)
            for rows in UNITS:
                s0 = Link(self.of(1 - h_me, True, rows), far.at[lo, rows], x_dev(1))
                s1 = Link(self.of(1 - h_me, False, rows), far.at[hi, rows], x_dev(3))
                s2 = Link(self.of(h_next, False, rows), near_a.at[hi, rows], x_dev(1, swap))
                s4 = Link(self.of(h_prev, True, rows), near_b.at[lo, rows], x_dev(3, swap))
                s3 = Link(self.of(h_next, True, rows), near_a.at[lo, rows], x_dev(1, swap))
                s5 = Link(self.of(h_prev, False, rows), near_b.at[hi, rows], x_dev(3, swap))
                when_owner.extend([s0, s1])
                when_relay.extend([s2, s4, s3, s5])
                self.links.append((s0, s1, s2, s3, s4, s5))

        def of(self, h, first, rows):
            return self.grad.at[pl.ds(h * 4 + (0 if first else 2), 2), rows]

        def send_far(self, u):
            s0, s1, _, _, _, _ = self.links[u]
            s0.start()
            s1.start()

        def send_near(self, u):
            _, _, s2, _, s4, _ = self.links[u]
            s2.start()
            s4.start()

        def middle(self, u):
            grad, far, rows = self.grad, self.far, UNITS[u]
            s0, s1, _, s3, _, s5 = self.links[u]
            for link, onward, h, first, k in ((s0, s3, h_next, True, 0), (s1, s5, h_prev, False, 2)):
                link.got(far.at[pl.ds(k, 2), rows])
                for j in (0, 1):
                    at = h * 4 + (0 if first else 2) + j
                    grad[at, rows] = (grad[at, rows].astype(F32) + far[k + j, rows].astype(F32)).astype(BF)
                onward.start()

        def finish(self, u):
            _, _, s2, s3, s4, s5 = self.links[u]
            lo, hi, rows = pl.ds(0, 2), pl.ds(2, 2), UNITS[u]
            s2.got(near_a.at[hi, rows])
            s4.got(near_b.at[lo, rows])
            s3.got(near_a.at[lo, rows])
            s5.got(near_b.at[hi, rows])

    red_down = Reduce(grad_down, far_down, False)
    red_up = Reduce(grad_up, far_up, True)
    own_link = Link(grad_up.at[pl.ds(h_me * 4, 4)], own_up, partner)
    when_owner.append(own_link)
    not_owner = jnp.logical_not(owner)

    outer(cot, act, grad_down)

    @pl.when(owner)
    def _():
        red_down.send_far(0)
        red_down.send_far(1)

    @pl.when(not_owner)
    def _():
        red_down.send_near(0)
        red_down.send_near(1)

    downs.finish()

    bias_sum[...] = jnp.zeros_like(bias_sum)

    @pl.loop(0, GROUP // 256)
    def _(i):
        rows = pl.ds(aligned(i * 256, 256), 256)
        s = jnp.dot(cot[rows], down_all[...], preferred_element_type=F32) * gelu_d[rows]
        s = s.astype(BF)
        slope[rows] = s
        bias_sum[...] += jnp.sum(s.astype(F32), axis=0, keepdims=True)

    outer(normed, slope, grad_up)

    @pl.when(owner)
    def _():
        own_link.start()
        red_up.send_far(0)
        red_up.send_far(1)

    @pl.when(not_owner)
    def _():
        red_down.middle(0)
        red_up.send_near(0)

    def across(left, right, result):
        @pl.loop(0, GROUP // 256)
        def _(i):
            rows = pl.ds(aligned(i * 256, 256), 256)
            result[rows] = lax.dot_general(
                left[rows], right[...], (((1,), (1,)), ((), ())), preferred_element_type=F32
            ).astype(BF)

    class Scatter:
        def __init__(self, partial, core, far, near):
            self.partial, self.core, self.far, self.near = partial, core, far, near
            self.over = []
            for dy in (2, 1, 3, 0):
                there = lax.rem(y + dy, 4)
                self.over.append((dy, Link(slot(partial, dy, 1 - c), core.at[there], partner).start()))
            always.extend(link for _, link in self.over)

        def combine(self):
            partial, core = self.partial, self.core
            for dy, link in self.over:
                there = lax.rem(y + dy, 4)
                link.got(core.at[there])
                if dy == 0:
                    continue
                rows = pl.ds(aligned((there * 2 + c) * TOK, TOK), TOK)
                partial[rows] = (partial[rows].astype(F32) + core[there].astype(F32)).astype(BF)
                if dy == 2:
                    self.t0 = Link(slot(partial, 2, c, 0, 64), self.far.at[0], y_dev(1)).start()
                    self.t1 = Link(slot(partial, 2, c, 64, 64), self.far.at[1], y_dev(3)).start()
                elif dy == 1:
                    self.t2 = Link(slot(partial, 1, c, 64, 64), self.near.at[0, pl.ds(64, 64)], y_dev(1)).start()
                else:
                    self.t3 = Link(slot(partial, 3, c, 0, 64), self.near.at[1, pl.ds(0, 64)], y_dev(3)).start()
            always.extend([self.t0, self.t1, self.t2, self.t3])

        def middle(self):
            partial, far = self.partial, self.far
            for dy, lo, k, link in ((1, 0, 0, self.t0), (3, 64, 1, self.t1)):
                link.got(far.at[k])
                there = lax.rem(y + dy, 4)
                rows = pl.ds(aligned((there * 2 + c) * TOK + lo, 16), 64)
                partial[rows] = (partial[rows].astype(F32) + far[k].astype(F32)).astype(BF)
                onward = Link(slot(partial, dy, c, lo, 64), self.near.at[k, pl.ds(lo, 64)], y_dev(dy)).start()
                always.append(onward)
                if k == 0:
                    self.t4 = onward
                else:
                    self.t5 = onward

        def finish(self):
            near = self.near
            self.t2.got(near.at[0, pl.ds(64, 64)])
            self.t3.got(near.at[1, pl.ds(0, 64)])
            self.t4.got(near.at[0, pl.ds(0, 64)])
            self.t5.got(near.at[1, pl.ds(64, 64)])
            own = self.partial[own_rows].astype(F32) + self.core[y].astype(F32)
            return own + near[0].astype(F32) + near[1].astype(F32)

    across(slope, up_all, part_back)
    sc_back = Scatter(part_back, core_back, far_back, near_back)

    @pl.when(not_owner)
    def _():
        red_down.middle(1)
        red_up.send_near(1)

    across(act, down_all, part_out)
    sc_out = Scatter(part_out, core_out, far_out, near_out)
    sc_back.combine()

    @pl.when(not_owner)
    def _():
        red_up.middle(0)

    sc_back.middle()
    sc_out.combine()

    @pl.when(not_owner)
    def _():
        red_up.middle(1)

    back[...] = sc_back.finish()
    standard, inverse = spread()
    nb = back[...]
    rows_small = (
        (0, D // 128, jnp.sum(nb * standard, axis=0, keepdims=True)),
        (D // 128, D // 128, jnp.sum(nb, axis=0, keepdims=True)),
        (2 * (D // 128), HID // 128, bias_sum[...]),
    )
    small[...] = jnp.zeros_like(small)
    for first, length, row in rows_small:
        for i in range(length):
            small[first + i : first + i + 1, :] = row[:, 128 * i : 128 * (i + 1)]
    n_norm = 2 * (D // 128)
    small_over = Link(small, small_core, partner).start()
    always.append(small_over)
    scaled = nb * gain[...][None]
    back[...] = inverse * (
        scaled
        - jnp.mean(scaled, axis=1, keepdims=True)
        - standard * jnp.mean(scaled * standard, axis=1, keepdims=True)
    )
    put_back = pltpu.make_async_copy(back, out_back, local_sems.at[0])
    put_back.start()

    def load_own(rows, source):
        for k in range(8):
            j, lanes = k % 4, slice((k // 4) * CHUNK_COLS, (k // 4 + 1) * CHUNK_COLS)
            total = source(j, rows, lanes).astype(F32)
            total = total + near_a[j, rows, lanes].astype(F32) + near_b[j, rows, lanes].astype(F32)
            zsum[k, rows] = total.astype(BF)

    def at_z(d):
        return lax.rem(z + d, 8)

    def add_rows(k, rows, incoming):
        zsum[k, rows] = (zsum[k, rows].astype(F32) + incoming.astype(F32)).astype(BF)

    overs = []

    def along_z(u):
        rows = UNITS[u]
        head, tail = pl.ds(rows.start, 48), pl.ds(rows.start + 48, rows.size - 48)

        @pl.when(owner)
        def _():
            red_down.finish(u)
            load_own(rows, lambda j, rows, lanes: grad_down[h_me * 4 + j, rows, lanes])

        @pl.when(not_owner)
        def _():
            if u == 0:
                own_link.got(own_up)
            red_up.finish(u)
            load_own(rows, lambda j, rows, lanes: own_up[j, rows, lanes])

        def link(src, dst, device):
            made = Link(src, dst, device).start()
            always.append(made)
            return made

        f = link(zsum.at[at_z(4), head], z_near_a.at[0, head], z_dev(1))
        b = link(zsum.at[at_z(4), tail], z_near_b.at[0, tail], z_dev(7))
        yield
        for step in range(3):
            got_f, got_b = (head, tail) if step == 0 else (rows, rows)
            f.got(z_near_a.at[step, got_f])
            add_rows(at_z(3 - step), got_f, z_near_a[step, got_f])
            f = link(zsum.at[at_z(3 - step), rows], z_near_a.at[step + 1, rows], z_dev(1))
            b.got(z_near_b.at[step, got_b])
            add_rows(at_z(5 + step), got_b, z_near_b[step, got_b])
            b = link(zsum.at[at_z(5 + step), rows], z_near_b.at[step + 1, rows], z_dev(7))
            yield
        f.got(z_near_a.at[3, rows])
        b.got(z_near_b.at[3, rows])
        mine[z, rows] = (
            zsum[z, rows].astype(F32) + z_near_a[3, rows].astype(F32) + z_near_b[3, rows].astype(F32)
        ).astype(BF)

        def forward(k, rows, device):
            return link(mine.at[k, rows], mine.at[k, rows], device)

        def hand_over(k):
            overs.append((link(mine.at[k, rows], other.at[k, rows], partner), k, rows))

        f, b = forward(z, rows, z_dev(1)), forward(z, rows, z_dev(7))
        hand_over(z)
        yield
        for d in (1, 2, 3):
            f.got(mine.at[at_z(8 - d), rows])
            f = forward(at_z(8 - d), rows if d < 3 else head, z_dev(1))
            b.got(mine.at[at_z(d), rows])
            b = forward(at_z(d), rows if d < 3 else tail, z_dev(7))
            hand_over(at_z(8 - d))
            hand_over(at_z(d))
            yield
        f.got(mine.at[at_z(4), head])
        b.got(mine.at[at_z(4), tail])
        hand_over(at_z(4))
        yield

    def small_sums():
        small_over.got(small_core)
        keep = lax.broadcasted_iota(jnp.int32, small.shape, 0) < n_norm
        small_y[y] = small[...] + jnp.where(keep, small_core[...], 0.0)
        y_links = [Link(small_y.at[y], small_y.at[y], y_dev(d)).start() for d in (1, 2, 3)]
        yield
        for d, link in zip((1, 2, 3), y_links):
            link.got(small_y.at[lax.rem(y + 4 - d, 4)])
        ysum = small_y[0] + small_y[1] + small_y[2] + small_y[3]
        small_x[x] = jnp.where(keep, ysum, small[...])
        x_links = [Link(small_x.at[x], small_x.at[x], x_dev(d)).start() for d in (1, 2, 3)]
        yield
        for d, link in zip((1, 2, 3), x_links):
            link.got(small_x.at[lax.rem(x + 4 - d, 4)])
        small_z[z] = small_x[0] + small_x[1] + small_x[2] + small_x[3]
        z_links = [Link(small_z.at[z], small_z.at[z], z_dev(d)).start() for d in range(1, 8)]
        yield
        for d, link in zip(range(1, 8), z_links):
            link.got(small_z.at[at_z(8 - d)])
        total = small_z[0]
        for k in range(1, 8):
            total = total + small_z[k]
        small_total[0] = total
        last = Link(small_total.at[0], small_total.at[1], partner).start()
        always.extend([*y_links, *x_links, *z_links, last])
        yield
        last.got(small_total.at[1])
        yield

    first, second, sums = along_z(0), along_z(1), small_sums()
    next(first)
    next(sums)
    next(first)
    next(sums)
    sc_out.middle()
    next(first)
    next(sums)
    next(second)
    next(first)
    next(second)
    next(sums)
    next(first)
    next(second)
    next(first)
    next(second)
    next(sums)
    put_small = pltpu.make_async_copy(small_total, out_small, local_sems.at[4])
    put_small.start()
    next(first)
    next(second)
    proj[...] = sc_out.finish() + down_bias[...][None]
    put_proj = pltpu.make_async_copy(proj, out_proj, local_sems.at[1])
    put_proj.start()
    next(first)
    next(second)
    next(first)
    next(second)
    next(second)
    next(second)
    put_mine = pltpu.make_async_copy(mine, out_mine, local_sems.at[2])
    put_mine.start()
    for link, k, rows in overs:
        link.got(other.at[k, rows])
    put_other = pltpu.make_async_copy(other, out_other, local_sems.at[3])
    put_other.start()

    for link in always:
        link.sent()

    @pl.when(owner)
    def _():
        for link in when_owner:
            link.sent()

    @pl.when(jnp.logical_not(owner))
    def _():
        for link in when_relay:
            link.sent()

    for put in (put_back, put_proj, put_mine, put_other, put_small):
        put.wait()
    assert count[0] <= N_LINKS


N_LINKS = 192


def on_device(patches, norm_gain, norm_bias, up_weight, up_bias, down_weight, down_bias, cotangent):
    scaling = 1.0 / math.sqrt(TOK * 256)
    vmem = pl.BlockSpec(memory_space=pltpu.VMEM)
    hbm = pl.BlockSpec(memory_space=pl.ANY)

    def V(*shape, dtype=BF):
        return pltpu.VMEM(shape, dtype)

    proj, back, mine, other, small = pl.pallas_call(
        step_kernel,
        out_shape=(
            jax.ShapeDtypeStruct((TOK, D), F32),
            jax.ShapeDtypeStruct((TOK, D), F32),
            jax.ShapeDtypeStruct((8, CHUNK_ROWS, CHUNK_COLS), BF),
            jax.ShapeDtypeStruct((8, CHUNK_ROWS, CHUNK_COLS), BF),
            jax.ShapeDtypeStruct((2, 32, 128), F32),
        ),
        in_specs=[hbm, hbm, vmem, vmem, vmem, vmem, hbm, hbm],
        out_specs=[hbm] * 5,
        scratch_shapes=[
            V(TOK, D), V(GROUP, D), V(GROUP, D), V(D, HID), V(D, HID), V(HID, dtype=F32),
            V(GROUP, HID, dtype=F32), V(GROUP, HID), V(GROUP, HID),
            V(GROUP, D), V(GROUP, D), V(4, TOK, D), V(4, TOK, D),
            V(2, 64, D), V(2, 64, D), V(2, TOK, D), V(2, TOK, D),
            V(8, CHUNK_ROWS, HID), V(8, CHUNK_ROWS, HID), V(4, CHUNK_ROWS, HID), V(4, CHUNK_ROWS, HID),
            V(4, CHUNK_ROWS, HID), V(4, CHUNK_ROWS, HID), V(4, CHUNK_ROWS, HID),
            V(8, CHUNK_ROWS, CHUNK_COLS), V(4, CHUNK_ROWS, CHUNK_COLS), V(4, CHUNK_ROWS, CHUNK_COLS),
            V(8, CHUNK_ROWS, CHUNK_COLS), V(8, CHUNK_ROWS, CHUNK_COLS),
            V(TOK, D, dtype=F32), V(TOK, D, dtype=F32), V(1, HID, dtype=F32),
            V(32, 128, dtype=F32), V(32, 128, dtype=F32), V(4, 32, 128, dtype=F32),
            V(4, 32, 128, dtype=F32), V(8, 32, 128, dtype=F32), V(2, 32, 128, dtype=F32),
            pltpu.SemaphoreType.DMA((N_LINKS,)),
            pltpu.SemaphoreType.DMA((N_LINKS,)),
            pltpu.SemaphoreType.DMA((9,)),
        ],
        compiler_params=pltpu.CompilerParams(
            collective_id=0, has_side_effects=True, vmem_limit_bytes=63 * 1024 * 1024
        ),
    )(
        patches, cotangent, norm_gain, norm_bias, up_bias, down_bias,
        up_weight, down_weight.T,
    )

    owner = lax.axis_index("row_0") == lax.axis_index("dp_1")

    def whole(chunks):
        left, right = chunks.reshape(2, HALF, CHUNK_COLS)
        return jnp.concatenate([left, right], axis=1).astype(F32) * scaling

    up_grad = whole(jnp.where(owner, other, mine))
    down_grad = whole(jnp.where(owner, mine, other)).T
    small = small * scaling
    n = D // 128
    norm_grad = small[0, : 2 * n].reshape(2, D)
    bias_grad = jnp.where(owner, small[0], small[1])[2 * n : 2 * n + HID // 128].reshape(HID)
    output = proj + patches.astype(F32)
    patch_grad = back + cotangent.astype(F32)
    return output, patch_grad, up_grad, down_grad, bias_grad, norm_grad


def solution(mesh):
    split = Mesh(
        mesh.devices.reshape(8, 2, 2, 4, mesh.shape["col"]),
        ("dp_0", "dp_1", "row_0", "row_1", "col"),
    )
    return jax.shard_map(
        on_device,
        mesh=split,
        in_specs=(
            P(DP_ROW_COL, None), P(), P(), P("col", ROW), P(ROW), P(ROW, "col"), P(), P(DP_ROW_COL, None),
        ),
        out_specs=(
            P(DP_ROW_COL, None), P(DP_ROW_COL, None), P("col", ROW), P(ROW, "col"), P(ROW), P(),
        ),
        check_vma=False,
    )
```

time: 148 us -> 129 us (0.87)
  Pallas kernels: 135 us -> 120 us
  local copies, waits for them, and re-layouts: 6.01 us -> 0.86 us
    pallas_call x1, Pallas kernels: 135 us -> 120 us  [on_device(): pl.pallas_call(step_kernel, out_shape=(jax.ShapeDtypeStruct((TOK, D), F32...]
    broadcast_in_dim x4 -> x0, local copies, waits for them, and re-layouts: 5.15 us -> none  [the longest x1 1.29 us: on_device(): norm_gain[None]]
where the time goes in v2:
time: 129 us; the launch traced here: 128 us
  Pallas kernels  120 us (93%)
  other arithmetic  6.57 us (5%)
    pallas_call x1, Pallas kernels, on_device(): pl.pallas_call(step_kernel, out_shape=(jax.ShapeDtypeStruct((TOK, D), F32...  120 us
    add x1, other arithmetic, on_device(): patch_grad = back + cotangent.astype(F32)  2.69 us

profile of v2, /device:TPU:7, one launch (start us, length us, event | category | flops | bytes accessed | tf_op | source)
XLA Modules:
  0.0 128.1 jit_solution(90007681057772413)
XLA Ops:
  0.6 0.0 copy-start
  0.7 0.0 copy-start.1
  0.7 120.0 %shard_map.127 = (f32[128,1408]{1,0:T(8,128)}, f32[128,1408]{1,0:T(8,128)}, bf16[8,176,384]{2,1,0:T(8,128)(2,1)}, bf16[8,176,384]{2,1,0:T(8,128)(2,1)}, f32[2,32,128]{2,1,0:T(8,128)}) custom-call(bf16[128,1408]{1,0:T(8,128)(2,1)} %patches_in.1, bf16[128,1408]{1,0:T(8,128)(2,1)} %cotangent_in.1, f32[1408]{0:T(1024)} %gain.1, f32[1408]{0:T(1024)} %bias.1, ...), custom_call_target="tpu_custom_call" | custom-call | tf_op jit(solution)/shard_map/pallas_call | solution.py:654
  120.6 0.0 copy-done
  120.6 0.0 copy-done.1
  120.6 0.0 copy-start.4
  120.7 0.0 copy-start.2
  120.7 0.0 copy-start.3
  120.7 2.7 %convert_add_fusion = (f32[128,1408]{1,0:T(8,128)}, f32[128,1408]{1,0:T(8,128)}) fusion(f32[128,1408]{1,0:T(8,128)} %get-tuple-element.12, bf16[128,1408]{1,0:T(8,128)(2,1)S(1)} %copy-done.1, f32[128,1408]{1,0:T(8,128)} %get-tuple-element.11, bf16[128,1408]{1,0:T(8,128)(2,1)S(1)} %copy-done), kind=kLoop, calls=%fused_computation.4 | loop fusion | flops 720896 | bytes 3604480 | tf_op jit(solution)/shard_map/add | solution.py:702
  123.4 0.0 copy-done.4
  123.4 0.6 reshape_squeeze.3
  124.0 0.6 fusion
  124.6 0.0 copy-done.2
  124.6 0.0 copy-done.3
  124.6 0.2 broadcast_select_fusion
  124.8 0.2 fusion.1
  125.1 1.5 %multiply_bitcast_fusion = f32[768,704]{0,1:T(8,128)} fusion(bf16[704,384]{1,0:T(8,128)(2,1)S(1)} %bitcast.12, bf16[704,384]{1,0:T(8,128)(2,1)S(1)} %bitcast.11), kind=kLoop, calls=%fused_computation | loop fusion | flops 2703360 | bytes 3244032 | tf_op jit(solution)/shard_map/transpose | solution.py:696
  126.6 1.5 %convert_multiply_fusion = f32[704,768]{1,0:T(8,128)} fusion(bf16[704,384]{1,0:T(8,128)(2,1)S(1)} %bitcast.9, bf16[704,384]{1,0:T(8,128)(2,1)S(1)} %bitcast.10), kind=kLoop, calls=%fused_computation.1 | loop fusion | flops 2703360 | bytes 3244032 | tf_op jit(solution)/shard_map/mul | solution.py:693
  (3 shorter events, 0.0 us)
Async XLA Ops:
  0.6 120.0 %copy-start = (bf16[128,1408]{1,0:T(8,128)(2,1)S(1)}, bf16[128,1408]{1,0:T(8,128)(2,1)}, u32[]{:S(2)}) copy-start(bf16[128,1408]{1,0:T(8,128)(2,1)} %patches_in.1) | copy-start | bytes 1081348
  0.7 120.0 %copy-start.1 = (bf16[128,1408]{1,0:T(8,128)(2,1)S(1)}, bf16[128,1408]{1,0:T(8,128)(2,1)}, u32[]{:S(2)}) copy-start(bf16[128,1408]{1,0:T(8,128)(2,1)} %cotangent_in.1) | copy-start | bytes 1081348
  120.6 2.7 %copy-start.4 = (f32[2,32,128]{2,1,0:T(8,128)S(1)}, f32[2,32,128]{2,1,0:T(8,128)}, u32[]{:S(2)}) copy-start(f32[2,32,128]{2,1,0:T(8,128)} %get-tuple-element.15) | copy-start | bytes 98308
  120.7 4.0 %copy-start.2 = (bf16[8,176,384]{2,1,0:T(8,128)(2,1)S(1)}, bf16[8,176,384]{2,1,0:T(8,128)(2,1)}, u32[]{:S(2)}) copy-start(bf16[8,176,384]{2,1,0:T(8,128)(2,1)} %get-tuple-element.14) | copy-start | bytes 3244036
  120.7 3.9 %copy-start.3 = (bf16[8,176,384]{2,1,0:T(8,128)(2,1)S(1)}, bf16[8,176,384]{2,1,0:T(8,128)(2,1)}, u32[]{:S(2)}) copy-start(bf16[8,176,384]{2,1,0:T(8,128)(2,1)} %get-tuple-element.13) | copy-start | bytes 3244036

commit v3 on v2

--- a/solution.py
+++ b/solution.py
@@ -37,10 +37,10 @@
     out_proj, out_back, out_mine, out_other, out_small,
     patches, normed, cot, up_all, down_all, bias_all, gelu_d, act, slope,
     part_out, part_back, core_out, core_back, far_out, far_back, near_out, near_back,
-    grad_up, grad_down, far_up, far_down, own_up, near_a, near_b,
-    zsum, z_near_a, z_near_b, mine, other,
+    grad_up, grad_down, swap_up, half_up, far_up, far_down, own_up, near_a, near_b, near_ua, near_ub,
+    zsum, usum, z_near_a, z_near_b, mine, other,
     proj, back, bias_sum, small, small_core, small_y, small_x, small_z, small_total,
-    send_sems, recv_sems, local_sems,
+    send_sems, recv_sems, local_sems, put_sems,
 ):
     z, c = lax.axis_index("dp_0"), lax.axis_index("dp_1")
     xl, y, xh = lax.axis_index("row_0"), lax.axis_index("row_1"), lax.axis_index("col")
@@ -79,6 +79,15 @@
     barrier = pltpu.get_barrier_semaphore()
     for peer in peers:
         pl.semaphore_signal(barrier, inc=1, device_id=peer, device_id_type=MESH)
+    def spread():
+        wide = patches[...].astype(F32)
+        centred = wide - jnp.mean(wide, axis=1, keepdims=True)
+        inverse = lax.rsqrt(jnp.mean(centred * centred, axis=1, keepdims=True) + EPSILON)
+        return centred * inverse, inverse
+
+    load_patches.wait()
+    normed[own_rows] = (spread()[0] * gain[...][None] + bias[...][None]).astype(BF)
+    load_cot.wait()
     pl.semaphore_wait(barrier, len(peers))
 
     count = [0]
@@ -211,26 +220,17 @@
             self.over_b = Link(slot(whole, 1, c), slot(whole, 1, c), partner).start()
             always.extend([self.far_a, self.over_a, self.far_b, self.over_b])
 
-        def finish(self):
+        def far(self):
             whole = self.whole
             self.far_a.got(slot(whole, 2, c, 0, 64))
             self.far_b.got(slot(whole, 2, c, 64, 64))
             self.over_far = Link(slot(whole, 2, c), slot(whole, 2, c), partner).start()
             always.append(self.over_far)
-            self.over.got(slot(whole, 0, 1 - c))
-            self.over_a.got(slot(whole, 3, 1 - c))
-            self.over_b.got(slot(whole, 1, 1 - c))
-            self.over_far.got(slot(whole, 2, 1 - c))
-
-    def spread():
-        wide = patches[...].astype(F32)
-        centred = wide - jnp.mean(wide, axis=1, keepdims=True)
-        inverse = lax.rsqrt(jnp.mean(centred * centred, axis=1, keepdims=True) + EPSILON)
-        return centred * inverse, inverse
-
-    load_cot.wait()
-    load_patches.wait()
-    normed[own_rows] = (spread()[0] * gain[...][None] + bias[...][None]).astype(BF)
+
+        def from_partner(self, dy):
+            name = ("over", "over_b", "over_far", "over_a")[dy]
+            getattr(self, name).got(slot(self.whole, dy, 1 - c))
+
     tok_n = Tokens(normed.at[own_rows], normed)
     tok_c = Tokens(cot.at[own_rows], cot)
 
@@ -260,12 +260,11 @@
     def _():
         downs.relay_last()
 
-    tok_n.finish()
-    ups.finish()
-
-    @pl.loop(0, GROUP // 256)
-    def _(i):
-        rows = pl.ds(aligned(i * 256, 256), 256)
+    def rows_of(dy):
+        return pl.ds(aligned(lax.rem(y + dy, 4) * 256, 256), 256)
+
+    def forward_block(dy):
+        rows = rows_of(dy)
         v = jnp.dot(normed[rows], up_all[...], preferred_element_type=F32) + bias_all[...][None]
         inner = jnp.tanh(GELU_ROOT * (v + GELU_CUBIC * v * v * v))
         act[rows] = (0.5 * v * (1.0 + inner)).astype(BF)
@@ -273,7 +272,36 @@
             1.0 + 3.0 * GELU_CUBIC * v * v
         )
 
-    tok_c.finish()
+    def slope_block(dy):
+        rows = rows_of(dy)
+        s = jnp.dot(cot[rows], down_all[...], preferred_element_type=F32) * gelu_d[rows]
+        s = s.astype(BF)
+        slope[rows] = s
+        bias_sum[...] += jnp.sum(s.astype(F32), axis=0, keepdims=True)
+
+    ups.finish()
+    tok_n.far()
+    for dy in (0, 3, 1):
+        tok_n.from_partner(dy)
+
+    @pl.loop(0, 3)
+    def _(i):
+        forward_block(lax.rem(i + 3, 4))
+
+    tok_c.far()
+    tok_n.from_partner(2)
+    forward_block(2)
+
+    downs.finish()
+    bias_sum[...] = jnp.zeros_like(bias_sum)
+    for dy in (0, 3, 1):
+        tok_c.from_partner(dy)
+
+    @pl.loop(0, 3)
+    def _(i):
+        slope_block(lax.rem(i + 3, 4))
+
+    tok_c.from_partner(2)
 
     def outer(left, right, result):
         for lo, hi in ((0, 512), (512, 1024), (1024, D)):
@@ -287,8 +315,8 @@
                 block, lo = block[rows:], lo + rows
 
     class Reduce:
-        def __init__(self, grad, far, swap):
-            self.grad, self.far, self.links = grad, far, []
+        def __init__(self, grad, far, near_a, near_b, swap):
+            self.grad, self.far, self.near, self.links = grad, far, (near_a, near_b), []
             lo, hi = pl.ds(0, 2), pl.ds(2, 2)
             for rows in UNITS:
                 s0 = Link(self.of(1 - h_me, True, rows), far.at[lo, rows], x_dev(1))
@@ -327,15 +355,18 @@
         def finish(self, u):
             _, _, s2, s3, s4, s5 = self.links[u]
             lo, hi, rows = pl.ds(0, 2), pl.ds(2, 2), UNITS[u]
+            near_a, near_b = self.near
             s2.got(near_a.at[hi, rows])
             s4.got(near_b.at[lo, rows])
             s3.got(near_a.at[lo, rows])
             s5.got(near_b.at[hi, rows])
 
-    red_down = Reduce(grad_down, far_down, False)
-    red_up = Reduce(grad_up, far_up, True)
-    own_link = Link(grad_up.at[pl.ds(h_me * 4, 4)], own_up, partner)
-    when_owner.append(own_link)
+    red_down = Reduce(grad_down, far_down, near_a, near_b, False)
+    red_up = Reduce(half_up, far_up, near_ua, near_ub, True)
+    own_links = []
+    for rows in UNITS:
+        own_links.append(Link(half_up.at[pl.ds(h_me * 4, 4), rows], own_up.at[pl.ds(0, 4), rows], partner))
+    when_owner.extend(own_links)
     not_owner = jnp.logical_not(owner)
 
     outer(cot, act, grad_down)
@@ -348,32 +379,178 @@
     @pl.when(not_owner)
     def _():
         red_down.send_near(0)
-        red_down.send_near(1)
-
-    downs.finish()
-
-    bias_sum[...] = jnp.zeros_like(bias_sum)
-
-    @pl.loop(0, GROUP // 256)
-    def _(i):
-        rows = pl.ds(aligned(i * 256, 256), 256)
-        s = jnp.dot(cot[rows], down_all[...], preferred_element_type=F32) * gelu_d[rows]
-        s = s.astype(BF)
-        slope[rows] = s
-        bias_sum[...] += jnp.sum(s.astype(F32), axis=0, keepdims=True)
-
+
+    slope_block(2)
     outer(normed, slope, grad_up)
 
-    @pl.when(owner)
-    def _():
-        own_link.start()
-        red_up.send_far(0)
-        red_up.send_far(1)
-
-    @pl.when(not_owner)
-    def _():
-        red_down.middle(0)
-        red_up.send_near(0)
+    swaps = []
+    for rows in UNITS:
+        pair = []
+        for h, d in ((0, 1), (1, 7)):
+            tiles = pl.ds(h * 4, 4)
+            pair.append(Link(grad_up.at[tiles, rows, lanes_z], swap_up.at[tiles, rows], z_dev(d)).start())
+        swaps.append(pair)
+        always.extend(pair)
+
+    def swapped(u):
+        rows = UNITS[u]
+        for h, swap in enumerate(swaps[u]):
+            swap.got(swap_up.at[pl.ds(h * 4, 4), rows])
+        for k in range(8):
+            half_up[k, rows] = (grad_up[k, rows, lanes_x].astype(F32) + swap_up[k, rows].astype(F32)).astype(BF)
+
+        @pl.when(owner)
+        def _():
+            own_links[u].start()
+            red_up.send_far(u)
+
+    def at_z(d):
+        return lax.rem(z + d, 8)
+
+    def add_rows(sums, k, rows, incoming):
+        sums[k, rows] = (sums[k, rows].astype(F32) + incoming.astype(F32)).astype(BF)
+
+    def link(src, dst, device):
+        made = Link(src, dst, device).start()
+        always.append(made)
+        return made
+
+    def held(src, dst, device, when):
+        made = Link(src, dst, device)
+        when.append(made)
+        return made
+
+    puts = []
+
+    class AlongZ:
+        def __init__(self, u):
+            self.u, self.rows = u, UNITS[u]
+            rows = self.rows
+            self.head = pl.ds(rows.start, 48)
+            self.tail = pl.ds(rows.start + 48, rows.size - 48)
+            self.down = []
+            for step in range(4):
+                f, b = (self.head, self.tail) if step == 0 else (rows, rows)
+                self.down.append((
+                    held(zsum.at[at_z(4 - step), f], z_near_a.at[step, f], z_dev(1), when_owner),
+                    held(zsum.at[at_z(4 + step), b], z_near_b.at[step, b], z_dev(7), when_owner),
+                ))
+            self.up = []
+            for step in range(2):
+                f, b = (self.head, self.tail) if step == 0 else (rows, rows)
+                to, fro = lax.div(at_z(4 - 2 * step), 2), lax.div(at_z(4 + 2 * step), 2)
+                self.up.append((
+                    held(usum.at[to, f], z_near_a.at[step, f], z_dev(2), when_relay),
+                    held(usum.at[fro, b], z_near_b.at[step, b], z_dev(6), when_relay),
+                ))
+            self.out = [
+                held(mine.at[z, rows], mine.at[z, rows], z_dev(1), always),
+                held(mine.at[z, rows], mine.at[z, rows], z_dev(7), always),
+                held(mine.at[z, rows], other.at[z, rows], partner, always),
+            ]
+
+        def begin_down(self):
+            red_down.finish(self.u)
+            for k in range(8):
+                j, lanes = k // 2, slice((k % 2) * CHUNK_COLS, (k % 2 + 1) * CHUNK_COLS)
+                total = grad_down[h_me * 4 + j, self.rows, lanes].astype(F32)
+                total = total + near_a[j, self.rows, lanes].astype(F32) + near_b[j, self.rows, lanes].astype(F32)
+                zsum[k, self.rows] = total.astype(BF)
+            for started in self.down[0]:
+                started.start()
+
+        def step_down(self, step):
+            got_f, got_b = (self.head, self.tail) if step == 0 else (self.rows, self.rows)
+            f, b = self.down[step]
+            f.got(z_near_a.at[step, got_f])
+            add_rows(zsum, at_z(3 - step), got_f, z_near_a[step, got_f])
+            self.down[step + 1][0].start()
+            b.got(z_near_b.at[step, got_b])
+            add_rows(zsum, at_z(5 + step), got_b, z_near_b[step, got_b])
+            self.down[step + 1][1].start()
+
+        def begin_up(self):
+            own_links[self.u].got(own_up.at[pl.ds(0, 4), self.rows])
+            red_up.finish(self.u)
+            for j in range(4):
+                total = own_up[j, self.rows].astype(F32)
+                total = total + near_ua[j, self.rows].astype(F32) + near_ub[j, self.rows].astype(F32)
+                usum[j, self.rows] = total.astype(BF)
+            for started in self.up[0]:
+                started.start()
+
+        def step_up(self):
+            f, b = self.up[0]
+            f.got(z_near_a.at[0, self.head])
+            add_rows(usum, lax.div(at_z(2), 2), self.head, z_near_a[0, self.head])
+            self.up[1][0].start()
+            b.got(z_near_b.at[0, self.tail])
+            add_rows(usum, lax.div(at_z(6), 2), self.tail, z_near_b[0, self.tail])
+            self.up[1][1].start()
+
+        def end(self, sums, at, links, k):
+            rows = self.rows
+            f, b = links
+            f.got(z_near_a.at[k, rows])
+            b.got(z_near_b.at[k, rows])
+            mine[z, rows] = (
+                sums[at, rows].astype(F32) + z_near_a[k, rows].astype(F32) + z_near_b[k, rows].astype(F32)
+            ).astype(BF)
+            for started in self.out:
+                started.start()
+
+        def end_down(self):
+            self.end(zsum, z, self.down[3], 3)
+
+        def end_up(self):
+            self.end(usum, lax.div(z, 2), self.up[1], 1)
+
+        def put(self, chunks, result, k):
+            row = lax.div(k, 2) * CHUNK_ROWS + self.rows.start
+            lane = lax.rem(k, 2) * CHUNK_COLS
+            there = result.at[pl.ds(aligned(row, 16), self.rows.size), pl.ds(aligned(lane, 128), CHUNK_COLS)]
+            copy = pltpu.make_async_copy(chunks.at[k, self.rows], there, put_sems.at[len(puts)])
+            copy.start()
+            puts.append(copy)
+
+        def spread(self):
+            rows = self.rows
+            overs = [(self.out[2], z)]
+            f, b = self.out[:2]
+            self.put(mine, out_mine, z)
+
+            def pass_on(k, rows, device):
+                return link(mine.at[k, rows], mine.at[k, rows], device)
+
+            def hand_over(k):
+                overs.append((link(mine.at[k, rows], other.at[k, rows], partner), k))
+
+            def take_over(count):
+                for _ in range(count):
+                    sent, k = overs.pop(0)
+                    sent.got(other.at[k, rows])
+                    self.put(other, out_other, k)
+
+            for d in (1, 2, 3):
+                f.got(mine.at[at_z(8 - d), rows])
+                f = pass_on(at_z(8 - d), rows if d < 3 else self.head, z_dev(1))
+                b.got(mine.at[at_z(d), rows])
+                b = pass_on(at_z(d), rows if d < 3 else self.tail, z_dev(7))
+                hand_over(at_z(8 - d))
+                hand_over(at_z(d))
+                self.put(mine, out_mine, at_z(8 - d))
+                self.put(mine, out_mine, at_z(d))
+                yield
+            f.got(mine.at[at_z(4), self.head])
+            b.got(mine.at[at_z(4), self.tail])
+            hand_over(at_z(4))
+            self.put(mine, out_mine, at_z(4))
+            take_over(5)
+            yield
+            take_over(3)
+            yield
+
+    unit0, unit1 = AlongZ(0), AlongZ(1)
 
     def across(left, right, result):
         @pl.loop(0, GROUP // 256)
@@ -436,24 +613,52 @@
     across(slope, up_all, part_back)
     sc_back = Scatter(part_back, core_back, far_back, near_back)
 
+
     @pl.when(not_owner)
     def _():
-        red_down.middle(1)
-        red_up.send_near(1)
+        red_down.middle(0)
+        red_down.send_near(1)
 
     across(act, down_all, part_out)
     sc_out = Scatter(part_out, core_out, far_out, near_out)
+
+    swapped(0)
+
+    @pl.when(not_owner)
+    def _():
+        red_up.send_near(0)
+
     sc_back.combine()
 
     @pl.when(not_owner)
     def _():
+        red_down.middle(1)
+
+    swapped(1)
+
+    @pl.when(owner)
+    def _():
+        unit0.begin_down()
+
+    sc_back.middle()
+
+    @pl.when(owner)
+    def _():
+        unit0.step_down(0)
+
+    sc_out.combine()
+
+    @pl.when(owner)
+    def _():
+        unit1.begin_down()
+        unit0.step_down(1)
+        unit1.step_down(0)
+        unit0.step_down(2)
+
+    @pl.when(not_owner)
+    def _():
         red_up.middle(0)
-
-    sc_back.middle()
-    sc_out.combine()
-
-    @pl.when(not_owner)
-    def _():
+        red_up.send_near(1)
         red_up.middle(1)
 
     back[...] = sc_back.finish()
@@ -480,120 +685,63 @@
     put_back = pltpu.make_async_copy(back, out_back, local_sems.at[0])
     put_back.start()
 
-    def load_own(rows, source):
-        for k in range(8):
-            j, lanes = k % 4, slice((k // 4) * CHUNK_COLS, (k // 4 + 1) * CHUNK_COLS)
-            total = source(j, rows, lanes).astype(F32)
-            total = total + near_a[j, rows, lanes].astype(F32) + near_b[j, rows, lanes].astype(F32)
-            zsum[k, rows] = total.astype(BF)
-
-    def at_z(d):
-        return lax.rem(z + d, 8)
-
-    def add_rows(k, rows, incoming):
-        zsum[k, rows] = (zsum[k, rows].astype(F32) + incoming.astype(F32)).astype(BF)
-
-    overs = []
-
-    def along_z(u):
-        rows = UNITS[u]
-        head, tail = pl.ds(rows.start, 48), pl.ds(rows.start + 48, rows.size - 48)
-
-        @pl.when(owner)
-        def _():
-            red_down.finish(u)
-            load_own(rows, lambda j, rows, lanes: grad_down[h_me * 4 + j, rows, lanes])
-
-        @pl.when(not_owner)
-        def _():
-            if u == 0:
-                own_link.got(own_up)
-            red_up.finish(u)
-            load_own(rows, lambda j, rows, lanes: own_up[j, rows, lanes])
-
-        def link(src, dst, device):
-            made = Link(src, dst, device).start()
-            always.append(made)
-            return made
-
-        f = link(zsum.at[at_z(4), head], z_near_a.at[0, head], z_dev(1))
-        b = link(zsum.at[at_z(4), tail], z_near_b.at[0, tail], z_dev(7))
+    def small_sums():
+        keep = lax.broadcasted_iota(jnp.int32, small.shape, 0) < n_norm
+        small_over.got(small_core)
+        small_z[z] = small[...] + jnp.where(keep, small_core[...], 0.0)
+        z_links = [link(small_z.at[z], small_z.at[z], z_dev(d)) for d in range(1, 8)]
         yield
-        for step in range(3):
-            got_f, got_b = (head, tail) if step == 0 else (rows, rows)
-            f.got(z_near_a.at[step, got_f])
-            add_rows(at_z(3 - step), got_f, z_near_a[step, got_f])
-            f = link(zsum.at[at_z(3 - step), rows], z_near_a.at[step + 1, rows], z_dev(1))
-            b.got(z_near_b.at[step, got_b])
-            add_rows(at_z(5 + step), got_b, z_near_b[step, got_b])
-            b = link(zsum.at[at_z(5 + step), rows], z_near_b.at[step + 1, rows], z_dev(7))
-            yield
-        f.got(z_near_a.at[3, rows])
-        b.got(z_near_b.at[3, rows])
-        mine[z, rows] = (
-            zsum[z, rows].astype(F32) + z_near_a[3, rows].astype(F32) + z_near_b[3, rows].astype(F32)
-        ).astype(BF)
-
-        def forward(k, rows, device):
-            return link(mine.at[k, rows], mine.at[k, rows], device)
-
-        def hand_over(k):
-            overs.append((link(mine.at[k, rows], other.at[k, rows], partner), k, rows))
-
-        f, b = forward(z, rows, z_dev(1)), forward(z, rows, z_dev(7))
-        hand_over(z)
-        yield
-        for d in (1, 2, 3):
-            f.got(mine.at[at_z(8 - d), rows])
-            f = forward(at_z(8 - d), rows if d < 3 else head, z_dev(1))
-            b.got(mine.at[at_z(d), rows])
-            b = forward(at_z(d), rows if d < 3 else tail, z_dev(7))
-            hand_over(at_z(8 - d))
-            hand_over(at_z(d))
-            yield
-        f.got(mine.at[at_z(4), head])
-        b.got(mine.at[at_z(4), tail])
-        hand_over(at_z(4))
-        yield
-
-    def small_sums():
-        small_over.got(small_core)
-        keep = lax.broadcasted_iota(jnp.int32, small.shape, 0) < n_norm
-        small_y[y] = small[...] + jnp.where(keep, small_core[...], 0.0)
-        y_links = [Link(small_y.at[y], small_y.at[y], y_dev(d)).start() for d in (1, 2, 3)]
-        yield
-        for d, link in zip((1, 2, 3), y_links):
-            link.got(small_y.at[lax.rem(y + 4 - d, 4)])
-        ysum = small_y[0] + small_y[1] + small_y[2] + small_y[3]
-        small_x[x] = jnp.where(keep, ysum, small[...])
-        x_links = [Link(small_x.at[x], small_x.at[x], x_dev(d)).start() for d in (1, 2, 3)]
-        yield
-        for d, link in zip((1, 2, 3), x_links):
-            link.got(small_x.at[lax.rem(x + 4 - d, 4)])
-        small_z[z] = small_x[0] + small_x[1] + small_x[2] + small_x[3]
-        z_links = [Link(small_z.at[z], small_z.at[z], z_dev(d)).start() for d in range(1, 8)]
-        yield
-        for d, link in zip(range(1, 8), z_links):
-            link.got(small_z.at[at_z(8 - d)])
+        for d, sent in zip(range(1, 8), z_links):
+            sent.got(small_z.at[at_z(8 - d)])
         total = small_z[0]
         for k in range(1, 8):
             total = total + small_z[k]
-        small_total[0] = total
-        last = Link(small_total.at[0], small_total.at[1], partner).start()
-        always.extend([*y_links, *x_links, *z_links, last])
+        small_y[y] = total
+        y_links = [link(small_y.at[y], small_y.at[y], y_dev(d)) for d in (1, 2, 3)]
+        yield
+        for d, sent in zip((1, 2, 3), y_links):
+            sent.got(small_y.at[lax.rem(y + 4 - d, 4)])
+        total = small_y[0] + small_y[1] + small_y[2] + small_y[3]
+        small_x[x] = jnp.where(keep, total, small_y[y])
+        x_links = [link(small_x.at[x], small_x.at[x], x_dev(d)) for d in (1, 2, 3)]
+        yield
+        for d, sent in zip((1, 2, 3), x_links):
+            sent.got(small_x.at[lax.rem(x + 4 - d, 4)])
+        small_total[0] = small_x[0] + small_x[1] + small_x[2] + small_x[3]
+        last = link(small_total.at[0], small_total.at[1], partner)
         yield
         last.got(small_total.at[1])
         yield
 
-    first, second, sums = along_z(0), along_z(1), small_sums()
-    next(first)
+    sums = small_sums()
+
+    @pl.when(owner)
+    def _():
+        unit1.step_down(1)
+        unit0.end_down()
+
+    @pl.when(not_owner)
+    def _():
+        unit0.begin_up()
+
+    sc_out.middle()
     next(sums)
-    next(first)
+
+    @pl.when(owner)
+    def _():
+        unit1.step_down(2)
+        unit1.end_down()
+
+    @pl.when(not_owner)
+    def _():
+        unit0.step_up()
+        unit1.begin_up()
+        unit0.end_up()
+        unit1.step_up()
+        unit1.end_up()
+
+    first, second = unit0.spread(), unit1.spread()
     next(sums)
-    sc_out.middle()
-    next(first)
-    next(sums)
-    next(second)
     next(first)
     next(second)
     next(sums)
@@ -602,25 +750,17 @@
     next(first)
     next(second)
     next(sums)
-    put_small = pltpu.make_async_copy(small_total, out_small, local_sems.at[4])
-    put_small.start()
-    next(first)
-    next(second)
     proj[...] = sc_out.finish() + down_bias[...][None]
     put_proj = pltpu.make_async_copy(proj, out_proj, local_sems.at[1])
     put_proj.start()
     next(first)
     next(second)
+
+    next(sums)
+    put_small = pltpu.make_async_copy(small_total, out_small, local_sems.at[4])
+    put_small.start()
     next(first)
     next(second)
-    next(second)
-    next(second)
-    put_mine = pltpu.make_async_copy(mine, out_mine, local_sems.at[2])
-    put_mine.start()
-    for link, k, rows in overs:
-        link.got(other.at[k, rows])
-    put_other = pltpu.make_async_copy(other, out_other, local_sems.at[3])
-    put_other.start()
 
     for link in always:
         link.sent()
@@ -635,7 +775,7 @@
         for link in when_relay:
             link.sent()
 
-    for put in (put_back, put_proj, put_mine, put_other, put_small):
+    for put in (put_back, put_proj, put_small, *puts):
         put.wait()
     assert count[0] <= N_LINKS
 
@@ -656,8 +796,8 @@
         out_shape=(
             jax.ShapeDtypeStruct((TOK, D), F32),
             jax.ShapeDtypeStruct((TOK, D), F32),
-            jax.ShapeDtypeStruct((8, CHUNK_ROWS, CHUNK_COLS), BF),
-            jax.ShapeDtypeStruct((8, CHUNK_ROWS, CHUNK_COLS), BF),
+            jax.ShapeDtypeStruct((HALF, HID), BF),
+            jax.ShapeDtypeStruct((HALF, HID), BF),
             jax.ShapeDtypeStruct((2, 32, 128), F32),
         ),
         in_specs=[hbm, hbm, vmem, vmem, vmem, vmem, hbm, hbm],
@@ -667,9 +807,11 @@
             V(GROUP, HID, dtype=F32), V(GROUP, HID), V(GROUP, HID),
             V(GROUP, D), V(GROUP, D), V(4, TOK, D), V(4, TOK, D),
             V(2, 64, D), V(2, 64, D), V(2, TOK, D), V(2, TOK, D),
-            V(8, CHUNK_ROWS, HID), V(8, CHUNK_ROWS, HID), V(4, CHUNK_ROWS, HID), V(4, CHUNK_ROWS, HID),
-            V(4, CHUNK_ROWS, HID), V(4, CHUNK_ROWS, HID), V(4, CHUNK_ROWS, HID),
-            V(8, CHUNK_ROWS, CHUNK_COLS), V(4, CHUNK_ROWS, CHUNK_COLS), V(4, CHUNK_ROWS, CHUNK_COLS),
+            V(8, CHUNK_ROWS, HID), V(8, CHUNK_ROWS, HID), V(8, CHUNK_ROWS, CHUNK_COLS), V(8, CHUNK_ROWS, CHUNK_COLS),
+            V(4, CHUNK_ROWS, CHUNK_COLS), V(4, CHUNK_ROWS, HID), V(4, CHUNK_ROWS, CHUNK_COLS),
+            V(4, CHUNK_ROWS, HID), V(4, CHUNK_ROWS, HID), V(4, CHUNK_ROWS, CHUNK_COLS), V(4, CHUNK_ROWS, CHUNK_COLS),
+            V(8, CHUNK_ROWS, CHUNK_COLS), V(4, CHUNK_ROWS, CHUNK_COLS),
+            V(4, CHUNK_ROWS, CHUNK_COLS), V(4, CHUNK_ROWS, CHUNK_COLS),
             V(8, CHUNK_ROWS, CHUNK_COLS), V(8, CHUNK_ROWS, CHUNK_COLS),
             V(TOK, D, dtype=F32), V(TOK, D, dtype=F32), V(1, HID, dtype=F32),
             V(32, 128, dtype=F32), V(32, 128, dtype=F32), V(4, 32, 128, dtype=F32),
@@ -677,6 +819,7 @@
             pltpu.SemaphoreType.DMA((N_LINKS,)),
             pltpu.SemaphoreType.DMA((N_LINKS,)),
             pltpu.SemaphoreType.DMA((9,)),
+            pltpu.SemaphoreType.DMA((32,)),
         ],
         compiler_params=pltpu.CompilerParams(
             collective_id=0, has_side_effects=True, vmem_limit_bytes=63 * 1024 * 1024
@@ -688,12 +831,8 @@
 
     owner = lax.axis_index("row_0") == lax.axis_index("dp_1")
 
-    def whole(chunks):
-        left, right = chunks.reshape(2, HALF, CHUNK_COLS)
-        return jnp.concatenate([left, right], axis=1).astype(F32) * scaling
-
-    up_grad = whole(jnp.where(owner, other, mine))
-    down_grad = whole(jnp.where(owner, mine, other)).T
+    up_grad = jnp.where(owner, other, mine).astype(F32) * scaling
+    down_grad = jnp.where(owner, mine, other).astype(F32).T * scaling
     small = small * scaling
     n = D // 128
     norm_grad = small[0, : 2 * n].reshape(2, D)

time: 129 us -> 114 us (0.88)
  Pallas kernels: 120 us -> 107 us
    pallas_call x1, Pallas kernels: 120 us -> 107 us  [on_device(): pl.pallas_call(step_kernel, out_shape=(jax.ShapeDtypeStruct((TOK, D), F32...]
    transpose x1 -> x0, other arithmetic: 1.53 us -> none  [on_device(): down_grad = whole(jnp.where(owner, mine, other)).T]
where the time goes in v3:
time: 114 us
  Pallas kernels  107 us (94%)
  other arithmetic  5.77 us (5%)
    pallas_call x1, Pallas kernels, on_device(): pl.pallas_call(step_kernel, out_shape=(jax.ShapeDtypeStruct((TOK, D), F32...  107 us
    add x1, other arithmetic, on_device(): patch_grad = back + cotangent.astype(F32)  2.69 us
    mul x1, other arithmetic, on_device(): down_grad = jnp.where(owner, mine, other).astype(F32).T * scaling  2.47 us

profile of v3, /device:TPU:7, one launch (start us, length us, event | category | flops | bytes accessed | tf_op | source)
XLA Modules:
  0.0 113.8 jit_solution(11582550951430223370)
XLA Ops:
  0.6 0.0 copy-start
  0.7 0.0 copy-start.1
  0.7 106.7 %shard_map.127 = (f32[128,1408]{1,0:T(8,128)}, f32[128,1408]{1,0:T(8,128)}, bf16[704,768]{1,0:T(8,128)(2,1)}, bf16[704,768]{1,0:T(8,128)(2,1)}, f32[2,32,128]{2,1,0:T(8,128)}) custom-call(bf16[128,1408]{1,0:T(8,128)(2,1)} %patches_in.1, bf16[128,1408]{1,0:T(8,128)(2,1)} %cotangent_in.1, f32[1408]{0:T(1024)} %gain.1, f32[1408]{0:T(1024)} %bias.1, ...), custom_call_target="tpu_custom_call" | custom-call | tf_op jit(solution)/shard_map/pallas_call | solution.py:794
  107.4 0.0 copy-done
  107.4 0.0 copy-done.1
  107.4 0.0 copy-start.4
  107.4 0.0 copy-start.2
  107.4 0.0 copy-start.3
  107.4 2.7 %convert_add_fusion = (f32[128,1408]{1,0:T(8,128)}, f32[128,1408]{1,0:T(8,128)}) fusion(f32[128,1408]{1,0:T(8,128)} %get-tuple-element.12, bf16[128,1408]{1,0:T(8,128)(2,1)S(1)} %copy-done.1, f32[128,1408]{1,0:T(8,128)} %get-tuple-element.11, bf16[128,1408]{1,0:T(8,128)(2,1)S(1)} %copy-done), kind=kLoop, calls=%fused_computation.2 | loop fusion | flops 720896 | bytes 3604480 | tf_op jit(solution)/shard_map/add | solution.py:841
  110.1 0.0 copy-done.4
  110.1 0.6 reshape_squeeze.3
  110.7 0.6 fusion
  111.3 0.0 copy-done.2
  111.3 0.0 copy-done.3
  111.3 2.5 %multiply_bitcast_fusion = (f32[768,704]{0,1:T(8,128)}, f32[704,768]{1,0:T(8,128)}) fusion(bf16[704,768]{1,0:T(8,128)(2,1)S(1)} %copy-done.2, bf16[704,768]{1,0:T(8,128)(2,1)S(1)} %copy-done.3, pred[]{:T(512)S(6)} %eq.3), kind=kLoop, calls=%fused_computation | loop fusion | flops 3244032 | bytes 6488065 | tf_op jit(solution)/shard_map/mul | solution.py:835
  (3 shorter events, 0.0 us)
Async XLA Ops:
  0.6 106.7 %copy-start = (bf16[128,1408]{1,0:T(8,128)(2,1)S(1)}, bf16[128,1408]{1,0:T(8,128)(2,1)}, u32[]{:S(2)}) copy-start(bf16[128,1408]{1,0:T(8,128)(2,1)} %patches_in.1) | copy-start | bytes 1081348
  0.7 106.7 %copy-start.1 = (bf16[128,1408]{1,0:T(8,128)(2,1)S(1)}, bf16[128,1408]{1,0:T(8,128)(2,1)}, u32[]{:S(2)}) copy-start(bf16[128,1408]{1,0:T(8,128)(2,1)} %cotangent_in.1) | copy-start | bytes 1081348
  107.4 2.7 %copy-start.4 = (f32[2,32,128]{2,1,0:T(8,128)S(1)}, f32[2,32,128]{2,1,0:T(8,128)}, u32[]{:S(2)}) copy-start(f32[2,32,128]{2,1,0:T(8,128)} %get-tuple-element.15) | copy-start | bytes 98308
  107.4 4.0 %copy-start.2 = (bf16[704,768]{1,0:T(8,128)(2,1)S(1)}, bf16[704,768]{1,0:T(8,128)(2,1)}, u32[]{:S(2)}) copy-start(bf16[704,768]{1,0:T(8,128)(2,1)} %get-tuple-element.14) | copy-start | bytes 3244036
  107.4 3.9 %copy-start.3 = (bf16[704,768]{1,0:T(8,128)(2,1)S(1)}, bf16[704,768]{1,0:T(8,128)(2,1)}, u32[]{:S(2)}) copy-start(bf16[704,768]{1,0:T(8,128)(2,1)} %get-tuple-element.13) | copy-start | bytes 3244036

commit v4 on v3

--- a/solution.py
+++ b/solution.py
@@ -725,7 +725,6 @@
         unit0.begin_up()
 
     sc_out.middle()
-    next(sums)
 
     @pl.when(owner)
     def _():
@@ -734,10 +733,10 @@
 
     @pl.when(not_owner)
     def _():
+        unit1.begin_up()
         unit0.step_up()
-        unit1.begin_up()
+        unit1.step_up()
         unit0.end_up()
-        unit1.step_up()
         unit1.end_up()
 
     first, second = unit0.spread(), unit1.spread()
@@ -747,6 +746,7 @@
     next(sums)
     next(first)
     next(second)
+    next(sums)
     next(first)
     next(second)
     next(sums)
@@ -777,10 +777,10 @@
 
     for put in (put_back, put_proj, put_small, *puts):
         put.wait()
-    assert count[0] <= N_LINKS
-
-
-N_LINKS = 192
+    assert count[0] == N_LINKS, count[0]
+
+
+N_LINKS = 162
 
 
 def on_device(patches, norm_gain, norm_bias, up_weight, up_bias, down_weight, down_bias, cotangent):

time: 114 us -> 113 us (level); the launches traced: 114 us -> 111 us
  Pallas kernels: 107 us -> 104 us
    pallas_call x1, Pallas kernels: 107 us -> 104 us  [on_device(): pl.pallas_call(step_kernel, out_shape=(jax.ShapeDtypeStruct((TOK, D), F32...]
where the time goes in v4:
time: 113 us; the launch traced here: 111 us
  Pallas kernels  104 us (92%)
  other arithmetic  5.77 us (5%)
    pallas_call x1, Pallas kernels, on_device(): pl.pallas_call(step_kernel, out_shape=(jax.ShapeDtypeStruct((TOK, D), F32...  104 us
    add x1, other arithmetic, on_device(): patch_grad = back + cotangent.astype(F32)  2.69 us
    mul x1, other arithmetic, on_device(): down_grad = jnp.where(owner, mine, other).astype(F32).T * scaling  2.47 us

profile of v4, /device:TPU:7, one launch (start us, length us, event | category | flops | bytes accessed | tf_op | source)
XLA Modules:
  0.0 111.5 jit_solution(4972872033543951491)
XLA Ops:
  0.6 0.0 copy-start
  0.7 0.0 copy-start.1
  0.7 104.3 %shard_map.127 = (f32[128,1408]{1,0:T(8,128)}, f32[128,1408]{1,0:T(8,128)}, bf16[704,768]{1,0:T(8,128)(2,1)}, bf16[704,768]{1,0:T(8,128)(2,1)}, f32[2,32,128]{2,1,0:T(8,128)}) custom-call(bf16[128,1408]{1,0:T(8,128)(2,1)} %patches_in.1, bf16[128,1408]{1,0:T(8,128)(2,1)} %cotangent_in.1, f32[1408]{0:T(1024)} %gain.1, f32[1408]{0:T(1024)} %bias.1, ...), custom_call_target="tpu_custom_call" | custom-call | tf_op jit(solution)/shard_map/pallas_call | solution.py:794
  105.0 0.0 copy-done
  105.0 0.0 copy-done.1
  105.0 0.0 copy-start.4
  105.0 0.0 copy-start.2
  105.0 0.0 copy-start.3
  105.0 2.7 %convert_add_fusion = (f32[128,1408]{1,0:T(8,128)}, f32[128,1408]{1,0:T(8,128)}) fusion(f32[128,1408]{1,0:T(8,128)} %get-tuple-element.12, bf16[128,1408]{1,0:T(8,128)(2,1)S(1)} %copy-done.1, f32[128,1408]{1,0:T(8,128)} %get-tuple-element.11, bf16[128,1408]{1,0:T(8,128)(2,1)S(1)} %copy-done), kind=kLoop, calls=%fused_computation.2 | loop fusion | flops 720896 | bytes 3604480 | tf_op jit(solution)/shard_map/add | solution.py:841
  107.7 0.0 copy-done.4
  107.8 0.6 reshape_squeeze.3
  108.4 0.6 fusion
  109.0 0.0 copy-done.2
  109.0 0.0 copy-done.3
  109.0 2.5 %multiply_bitcast_fusion = (f32[768,704]{0,1:T(8,128)}, f32[704,768]{1,0:T(8,128)}) fusion(bf16[704,768]{1,0:T(8,128)(2,1)S(1)} %copy-done.2, bf16[704,768]{1,0:T(8,128)(2,1)S(1)} %copy-done.3, pred[]{:T(512)S(6)} %eq.3), kind=kLoop, calls=%fused_computation | loop fusion | flops 3244032 | bytes 6488065 | tf_op jit(solution)/shard_map/mul | solution.py:835
  (3 shorter events, 0.0 us)
Async XLA Ops:
  0.6 104.4 %copy-start = (bf16[128,1408]{1,0:T(8,128)(2,1)S(1)}, bf16[128,1408]{1,0:T(8,128)(2,1)}, u32[]{:S(2)}) copy-start(bf16[128,1408]{1,0:T(8,128)(2,1)} %patches_in.1) | copy-start | bytes 1081348
  0.7 104.4 %copy-start.1 = (bf16[128,1408]{1,0:T(8,128)(2,1)S(1)}, bf16[128,1408]{1,0:T(8,128)(2,1)}, u32[]{:S(2)}) copy-start(bf16[128,1408]{1,0:T(8,128)(2,1)} %cotangent_in.1) | copy-start | bytes 1081348
  105.0 2.7 %copy-start.4 = (f32[2,32,128]{2,1,0:T(8,128)S(1)}, f32[2,32,128]{2,1,0:T(8,128)}, u32[]{:S(2)}) copy-start(f32[2,32,128]{2,1,0:T(8,128)} %get-tuple-element.15) | copy-start | bytes 98308
  105.0 4.0 %copy-start.2 = (bf16[704,768]{1,0:T(8,128)(2,1)S(1)}, bf16[704,768]{1,0:T(8,128)(2,1)}, u32[]{:S(2)}) copy-start(bf16[704,768]{1,0:T(8,128)(2,1)} %get-tuple-element.14) | copy-start | bytes 3244036
  105.0 3.9 %copy-start.3 = (bf16[704,768]{1,0:T(8,128)(2,1)S(1)}, bf16[704,768]{1,0:T(8,128)(2,1)}, u32[]{:S(2)}) copy-start(bf16[704,768]{1,0:T(8,128)(2,1)} %get-tuple-element.13) | copy-start | bytes 3244036
